TPU v7x, 32 devices: a 4x2x2 block of a 4x4x8 slice. The times are simulated.
32 devices in a mesh: dp: 4 (over y, z), fsdp: 8 (over x, core).
Axes of the slice: x: 4, y: 2, z: 2, core: 2. Of those that a mesh axis runs over, the one named last changes fastest.
The devices are a block of a 4x4x8 slice.
Arguments:
- tokens: bfloat16 [32, 128, 1024], P(('dp', 'fsdp')), parts along dimension 0
- lengths: int32 [32], P(('dp', 'fsdp')), parts along dimension 0
- attn_gain: bfloat16 [2, 1024], P(None, 'fsdp')
- w_q: bfloat16 [2, 1024, 1024], P(None, None, 'fsdp')
- w_k: bfloat16 [2, 1024, 1024], P(None, None, 'fsdp')
- w_v: bfloat16 [2, 1024, 1024], P(None, None, 'fsdp')
- w_o: bfloat16 [2, 1024, 1024], P(None, 'fsdp')
- rel_bias: bfloat16 [2, 32, 16], P(None, None, 'fsdp')
- ffn_gain: bfloat16 [2, 1024], P(None, 'fsdp')
- w_in0: bfloat16 [2, 1024, 2816], P(None, None, 'fsdp')
- w_in1: bfloat16 [2, 1024, 2816], P(None, None, 'fsdp')
- w_out: bfloat16 [2, 2816, 1024], P(None, 'fsdp')
- final_gain: bfloat16 [1024], P('fsdp')
Outputs:
- output: bfloat16 [32, 128, 1024], P(('dp', 'fsdp')), parts along dimension 0
There are 4 independent parts. A program takes and returns all parts, laid end to end along the dimension named above; an argument that names none is the same for every part.
All inputs are finite; a program needn't handle non-finite values.
Results may differ from a plain program's by a relative error of at most 0.0106357.
Values are sent between devices in bfloat16 or wider.
A program may use at most 768 MiB of HBM per device.

v0:
```python
import jax
import jax.numpy as jnp
from jax import lax
from jax.sharding import PartitionSpec as P

HEAD_DIM = 64
NUM_BUCKETS = 32
NORM_EPS = 1e-6


def bucket_table(seq_len):
    positions = jnp.arange(seq_len, dtype=jnp.int32)
    rel_pos = positions[None, :] - positions[:, None]
    half_buckets = NUM_BUCKETS // 2
    max_exact = half_buckets // 2
    distance = jnp.abs(rel_pos)
    log_steps = jnp.arange(1, half_buckets - max_exact, dtype=jnp.int32)
    thresholds = max_exact * max_exact * 2 ** log_steps
    log_bucket = max_exact + jnp.sum((distance * distance)[:, :, None] >= thresholds, axis=-1, dtype=jnp.int32)
    return jnp.where(rel_pos > 0, half_buckets, 0) + jnp.where(distance < max_exact, distance, log_bucket)


def rms_norm(hidden, gain):
    mean_sq = jnp.mean(hidden * hidden, axis=-1, keepdims=True)
    return (hidden * lax.rsqrt(mean_sq + NORM_EPS) * gain.astype(jnp.float32)).astype(jnp.bfloat16)


def attention_block(normed, w_q, w_k, w_v, w_o, bias_table, key_ok, buckets):
    num_prompts = normed.shape[0]
    seq_len = normed.shape[1]
    num_heads = w_q.shape[1] // HEAD_DIM

    def project(weight):
        projected = jnp.einsum("bsd,dn->bsn", normed, weight, preferred_element_type=jnp.float32)
        return projected.astype(jnp.bfloat16).reshape(num_prompts, seq_len, num_heads, HEAD_DIM)

    queries = project(w_q)
    keys_proj = project(w_k)
    values = project(w_v)
    scores = jnp.einsum("bqhd,bkhd->bhqk", queries, keys_proj, preferred_element_type=jnp.float32)
    pos_bias = jnp.take(bias_table.T, buckets, axis=1).astype(jnp.float32)
    scores = jnp.where(key_ok[:, None, None, :], scores + pos_bias[None], -1e30)
    attn_probs = jax.nn.softmax(scores, axis=-1).astype(jnp.bfloat16)
    context = jnp.einsum("bhqk,bkhd->bqhd", attn_probs, values, preferred_element_type=jnp.float32)
    context = context.astype(jnp.bfloat16).reshape(num_prompts, seq_len, num_heads * HEAD_DIM)
    return jnp.einsum("bsn,nd->bsd", context, w_o, preferred_element_type=jnp.float32)


def ffn_block(normed, w_in0, w_in1, w_out):
    gate_act = jnp.einsum("bsd,df->bsf", normed, w_in0, preferred_element_type=jnp.float32)
    lin_act = jnp.einsum("bsd,df->bsf", normed, w_in1, preferred_element_type=jnp.float32)
    mixed_act = (jax.nn.gelu(gate_act, approximate=True) * lin_act).astype(jnp.bfloat16)
    return jnp.einsum("bsf,fd->bsd", mixed_act, w_out, preferred_element_type=jnp.float32)


def solution(mesh):
    batch_spec = P(("dp", "fsdp"))
    col_spec = P(None, None, "fsdp")
    row_spec = P(None, "fsdp", None)
    gain_spec = P(None, "fsdp")
    in_specs = (batch_spec, batch_spec, gain_spec, col_spec, col_spec, col_spec, row_spec, col_spec, gain_spec, col_spec, col_spec, row_spec, P("fsdp"))

    def local_forward(tokens, lengths, attn_gain, w_q, w_k, w_v, w_o, rel_bias, ffn_gain, w_in0, w_in1, w_out, final_gain):
        seq_len = tokens.shape[1]
        buckets = bucket_table(seq_len)
        key_ok = jnp.arange(seq_len, dtype=jnp.int32)[None, :] < lengths[:, None]
        hidden = tokens.astype(jnp.float32)
        for layer_idx in range(w_q.shape[0]):
            gain_full = lax.all_gather(attn_gain[layer_idx], "fsdp", axis=0, tiled=True)
            wq_full = lax.all_gather(w_q[layer_idx], "fsdp", axis=1, tiled=True)
            wk_full = lax.all_gather(w_k[layer_idx], "fsdp", axis=1, tiled=True)
            wv_full = lax.all_gather(w_v[layer_idx], "fsdp", axis=1, tiled=True)
            wo_full = lax.all_gather(w_o[layer_idx], "fsdp", axis=0, tiled=True)
            table_full = lax.all_gather(rel_bias[layer_idx], "fsdp", axis=1, tiled=True)
            normed = rms_norm(hidden, gain_full)
            hidden = hidden + attention_block(normed, wq_full, wk_full, wv_full, wo_full, table_full, key_ok, buckets)
            gain_full = lax.all_gather(ffn_gain[layer_idx], "fsdp", axis=0, tiled=True)
            wi0_full = lax.all_gather(w_in0[layer_idx], "fsdp", axis=1, tiled=True)
            wi1_full = lax.all_gather(w_in1[layer_idx], "fsdp", axis=1, tiled=True)
            wout_full = lax.all_gather(w_out[layer_idx], "fsdp", axis=0, tiled=True)
            normed = rms_norm(hidden, gain_full)
            hidden = hidden + ffn_block(normed, wi0_full, wi1_full, wout_full)
        final_full = lax.all_gather(final_gain, "fsdp", axis=0, tiled=True)
        normed_out = rms_norm(hidden, final_full)
        return jnp.where(key_ok[:, :, None], normed_out, jnp.zeros_like(normed_out))

    return jax.shard_map(local_forward, mesh=mesh, in_specs=in_specs, out_specs=batch_spec, check_vma=False)
```

profile of v0, /device:TPU:81, one launch (start us, length us, event | category | flops | bytes accessed | tf_op | source)
XLA Modules:
  0.0 451.1 jit_solution(16905788159005754176)
XLA Ops:
  6.6 2.0 fusion.152
  8.7 2.0 fusion.151
  10.7 0.8 fusion.153
  11.7 0.8 fusion.150
  12.7 1.2 fusion.148
  14.3 1.2 fusion.147
  15.7 1.2 fusion.149
  17.0 0.7 all-gather.52.cloned.1.call-update
  17.9 0.7 all-gather.54.cloned.1.call-update
  18.6 0.6 all-gather.50.cloned.1.call-update
  19.3 0.7 all-gather.56.cloned.1.call-update
  20.1 0.6 all-gather.58.cloned.1.call-update
  20.7 0.7 all-gather.60.cloned.1.call-update
  22.1 12.3 %all-gather = bf16[1,1024]{1,0:T(2,128)(2,1)S(1)} all-gather(bf16[1,128]{1,0:T(2,128)(2,1)S(1)} %get-tuple-element.25), channel_id=2, replica_groups=mesh['dp'=4,'fsdp'=8] {'fsdp'}, dimensions={1}, use_global_device_ids=true | all-gather | bytes 2304 | tf_op jit(solution)/shard_map/all_gather | solution.py:69
  34.5 8.2 %all-gather.4 = bf16[1,32,16]{1,0,2:T(2,128)(2,1)S(1)} all-gather(bf16[1,32,2]{1,0,2:T(2,128)(2,1)S(1)} %copy.83), channel_id=6, replica_groups=mesh['dp'=4,'fsdp'=8] {'fsdp'}, dimensions={2}, use_global_device_ids=true | all-gather | bytes 1152 | tf_op jit(solution)/shard_map/all_gather | solution.py:74
  43.1 57.8 %gather_fusion = bf16[16384,16]{1,0:T(8,128)(2,1)} fusion(bf16[16,32]{0,1:T(8,128)(2,1)S(1)} %bitcast.189, s32[16384]{0:T(1024)S(1)} %bitcast_clamp_fusion), kind=kCustom, calls=%fused_computation.clone | custom fusion | bytes 1114112 | tf_op jit(solution)/shard_map/jit(_take)/gather | solution.py:41
  100.8 6.5 %copy.66 = bf16[128,128,16]{0,1,2:T(8,128)(2,1)S(1)} copy(bf16[128,128,16]{2,1,0:T(8,128)(2,1)} %bitcast.192) | data formatting | bytes 1048576 | tf_op jit(solution)/shard_map/jit(_take)/gather | solution.py:41
  108.2 9.5 %all-gather.6 = bf16[1,1024]{1,0:T(2,128)(2,1)S(1)} all-gather(bf16[1,128]{1,0:T(2,128)(2,1)S(1)} %get-tuple-element.23), channel_id=8, replica_groups=mesh['dp'=4,'fsdp'=8] {'fsdp'}, dimensions={1}, use_global_device_ids=true | all-gather | bytes 2304 | tf_op jit(solution)/shard_map/all_gather | solution.py:77
  117.8 0.6 convert_element_type.131
  118.4 8.2 %all-gather.10 = bf16[1,1024]{1,0:T(2,128)(2,1)S(1)} all-gather(bf16[1,128]{1,0:T(2,128)(2,1)S(1)} %get-tuple-element.24), channel_id=12, replica_groups=mesh['dp'=4,'fsdp'=8] {'fsdp'}, dimensions={1}, use_global_device_ids=true | all-gather | bytes 2304 | tf_op jit(solution)/shard_map/all_gather | solution.py:69
  126.6 0.6 convert_element_type.132
  127.2 9.6 %all-gather.14 = bf16[1,32,16]{1,0,2:T(2,128)(2,1)S(1)} all-gather(bf16[1,32,2]{1,0,2:T(2,128)(2,1)S(1)} %copy.84), channel_id=16, replica_groups=mesh['dp'=4,'fsdp'=8] {'fsdp'}, dimensions={2}, use_global_device_ids=true | all-gather | bytes 1152 | tf_op jit(solution)/shard_map/all_gather | solution.py:74
  136.9 57.8 %gather_fusion.1 = bf16[16384,16]{1,0:T(8,128)(2,1)} fusion(bf16[16,32]{0,1:T(8,128)(2,1)S(1)} %bitcast.190, s32[16384]{0:T(1024)S(1)} %bitcast_clamp_fusion), kind=kCustom, calls=%fused_computation.1.clone | custom fusion | bytes 1114112 | tf_op jit(solution)/shard_map/jit(_take)/gather | solution.py:41
  194.7 6.5 %copy.75 = bf16[128,128,16]{0,1,2:T(8,128)(2,1)S(1)} copy(bf16[128,128,16]{2,1,0:T(8,128)(2,1)} %bitcast.191) | data formatting | bytes 1048576 | tf_op jit(solution)/shard_map/jit(_take)/gather | solution.py:41
  201.2 8.3 %all-gather.16 = bf16[1,1024]{1,0:T(2,128)(2,1)S(1)} all-gather(bf16[1,128]{1,0:T(2,128)(2,1)S(1)} %get-tuple-element.22), channel_id=18, replica_groups=mesh['dp'=4,'fsdp'=8] {'fsdp'}, dimensions={1}, use_global_device_ids=true | all-gather | bytes 2304 | tf_op jit(solution)/shard_map/all_gather | solution.py:77
  209.5 0.6 convert_element_type.133
  210.1 9.8 %all-gather.20 = bf16[8,1,128]{2,1,0:T(2,128)(2,1)S(1)} all-gather(bf16[1,1,128]{2,1,0:T(2,128)(2,1)S(1)} %bitcast.210), channel_id=1, replica_groups=mesh['dp'=4,'fsdp'=8] {'fsdp'}, dimensions={0}, use_global_device_ids=true | all-gather | bytes 2304 | tf_op jit(solution)/shard_map/all_gather | solution.py:83
  219.8 0.6 convert_element_type.134
  220.6 2.1 fusion.93
  222.9 2.1 fusion.96
  225.2 2.1 fusion.90
  228.5 2.1 multiply_reduce_fusion.3
  230.7 4.9 %fusion.50 = f32[128,2816]{1,0:T(8,128)S(1)} fusion(bf16[1,1024,2816]{1,2,0:T(8,128)(2,1)} %all-gather.44.cloned.1.call-done, f32[1,128,1024]{2,1,0:T(8,128)S(1)} %get-tuple-element.27, f32[1024]{0:T(1024)S(1)} %bitcast.208, f32[128]{0:T(128)S(1)} %add_rsqrt_fusion.3), kind=kOutput, calls=%fused_computation.46 | convolution fusion | flops 741474304 | bytes 7737856 | tf_op jit(solution)/shard_map/bsd,df->bsf/dot_general | solution.py:50
  235.7 7.2 %multiply_reduce_fusion.2 = (f32[128]{0:T(128)S(1)}, f32[1,128,1024]{2,1,0:T(8,128)S(1)}) fusion(f32[1,128,1024]{2,1,0:T(8,128)S(1)} %get-tuple-element.27, bf16[1,2816,1024]{2,1,0:T(8,128)(2,1)} %all-gather.48.cloned.1.call-done, f32[128,2816]{1,0:T(8,128)S(1)} %fusion.50, bf16[1,1024,2816]{1,2,0:T(8,128)(2,1)} %all-gather.46.cloned.1.call-done, ...), kind=kOutput, calls=%fused_computation.88 | convolution fusion | flops 1477902208 | bytes 14029824 | tf_op jit(solution)/shard_map/bsf,fd->bsd/dot_general | solution.py:53
  243.1 6.1 %all-gather.52.cloned.1.call-done = bf16[1,1024,1024]{2,1,0:T(8,128)(2,1)} async-done(((bf16[1,1024,128]{2,1,0:T(8,128)(2,1)}), bf16[1,1024,1024]{2,1,0:T(8,128)(2,1)}) %all-gather.52.cloned.1.call-update) | async-done | bytes 2097168 | tf_op jit(solution)/shard_map/all_gather | solution.py:70
  249.2 2.0 fusion.102
  251.4 23.6 %all-gather.54.cloned.1.call-done = bf16[1,1024,1024]{2,1,0:T(8,128)(2,1)} async-done(((bf16[1,1024,128]{2,1,0:T(8,128)(2,1)}), bf16[1,1024,1024]{2,1,0:T(8,128)(2,1)}) %all-gather.54.cloned.1.call-update) | async-done | bytes 2097168 | tf_op jit(solution)/shard_map/all_gather | solution.py:71
  275.1 2.0 fusion.105
  277.3 23.4 %all-gather.50.cloned.1.call-done = bf16[1,1024,1024]{2,1,0:T(8,128)(2,1)} async-done(((bf16[1,1024,128]{2,1,0:T(8,128)(2,1)}), bf16[1,1024,1024]{2,1,0:T(8,128)(2,1)}) %all-gather.50.cloned.1.call-update) | async-done | bytes 2097168 | tf_op jit(solution)/shard_map/all_gather | solution.py:72
  300.7 2.0 fusion.99
  304.0 21.3 %all-gather.56.cloned.1.call-done = bf16[1,1024,1024]{2,1,0:T(8,128)(2,1)} async-done(((bf16[1,128,1024]{2,1,0:T(8,128)(2,1)}), bf16[1,1024,1024]{2,1,0:T(8,128)(2,1)}) %all-gather.56.cloned.1.call-update) | async-done | bytes 2097168 | tf_op jit(solution)/shard_map/all_gather | solution.py:73
  325.3 2.1 multiply_reduce_fusion.1
  327.4 35.2 %all-gather.58.cloned.1.call-done = bf16[1,1024,2816]{1,2,0:T(8,128)(2,1)} async-done(((bf16[1,1024,352]{1,2,0:T(8,128)(2,1)}), bf16[1,1024,2816]{1,2,0:T(8,128)(2,1)}) %all-gather.58.cloned.1.call-update) | async-done | bytes 5767184 | tf_op jit(solution)/shard_map/all_gather | solution.py:78
  362.6 4.9 %fusion.59 = f32[128,2816]{1,0:T(8,128)S(1)} fusion(bf16[1,1024,2816]{1,2,0:T(8,128)(2,1)} %all-gather.58.cloned.1.call-done, f32[1,128,1024]{2,1,0:T(8,128)S(1)} %get-tuple-element.31, f32[1024]{0:T(1024)S(1)} %bitcast.205, f32[128]{0:T(128)S(1)} %add_rsqrt_fusion.1), kind=kOutput, calls=%fused_computation.53 | convolution fusion | flops 741474304 | bytes 7737856 | tf_op jit(solution)/shard_map/bsd,df->bsf/dot_general | solution.py:50
  367.6 32.1 %all-gather.60.cloned.1.call-done = bf16[1,1024,2816]{1,2,0:T(8,128)(2,1)} async-done(((bf16[1,1024,352]{1,2,0:T(8,128)(2,1)}), bf16[1,1024,2816]{1,2,0:T(8,128)(2,1)}) %all-gather.60.cloned.1.call-update) | async-done | bytes 5767184 | tf_op jit(solution)/shard_map/all_gather | solution.py:79
  399.6 36.9 %all-gather.62.cloned.1.call-done = bf16[1,2816,1024]{2,1,0:T(8,128)(2,1)} async-done(((bf16[1,352,1024]{2,1,0:T(8,128)(2,1)}), bf16[1,2816,1024]{2,1,0:T(8,128)(2,1)}) %all-gather.62.cloned.1.call-update) | async-done | bytes 5767184 | tf_op jit(solution)/shard_map/all_gather | solution.py:80
  436.5 7.2 %multiply_reduce_fusion = (f32[128]{0:T(128)S(1)}, f32[1,128,1024]{2,1,0:T(8,128)S(1)}) fusion(f32[1,128,1024]{2,1,0:T(8,128)S(1)} %get-tuple-element.31, bf16[1,2816,1024]{2,1,0:T(8,128)(2,1)} %all-gather.62.cloned.1.call-done, f32[128,2816]{1,0:T(8,128)S(1)} %fusion.59, bf16[1,1024,2816]{1,2,0:T(8,128)(2,1)} %all-gather.60.cloned.1.call-done, ...), kind=kOutput, calls=%fused_computation.84 | convolution fusion | flops 1477902208 | bytes 14029824 | tf_op jit(solution)/shard_map/bsf,fd->bsd/dot_general | solution.py:53
  443.8 0.8 fusion.124
  (95 shorter events, 6.0 us)
Async XLA Ops:
  6.5 4.2 copy-start.4
  6.5 5.2 %copy-start.5 = (bf16[2,128,1024]{2,1,0:T(8,128)(2,1)S(1)}, bf16[2,128,1024]{2,1,0:T(8,128)(2,1)}, u32[]{:S(2)}) copy-start(bf16[2,128,1024]{2,1,0:T(8,128)(2,1)} %param.21) | copy-start | bytes 1572868
  6.6 214.1 %all-gather.38.cloned.1.call-start = ((), (), s32[]{:S(2)}) async-start(), calls=%async_computation.1 | async-start | bytes 2359296 | tf_op jit(solution)/shard_map/all_gather | solution.py:70
  8.5 4.2 copy-start.1
  8.6 214.3 %all-gather.40.cloned.1.call-start = ((), (), s32[]{:S(2)}) async-start(), calls=%async_computation.2 | async-start | bytes 2359296 | tf_op jit(solution)/shard_map/all_gather | solution.py:71
  10.7 214.5 %all-gather.36.cloned.1.call-start = ((), (), s32[]{:S(2)}) async-start(), calls=%async_computation | async-start | bytes 2359296 | tf_op jit(solution)/shard_map/all_gather | solution.py:72
  11.6 216.9 %all-gather.42.cloned.1.call-start = ((), (), s32[]{:S(2)}) async-start(), calls=%async_computation.3 | async-start | bytes 2359296 | tf_op jit(solution)/shard_map/all_gather | solution.py:73
  12.5 1.8 copy-start.2
  12.6 218.1 %all-gather.44.cloned.1.call-start = ((), (), s32[]{:S(2)}) async-start(), calls=%async_computation.4 | async-start | bytes 6488064 | tf_op jit(solution)/shard_map/all_gather | solution.py:78
  13.9 1.7 copy-start.3
  14.0 221.7 %all-gather.46.cloned.1.call-start = ((), (), s32[]{:S(2)}) async-start(), calls=%async_computation.5 | async-start | bytes 6488064 | tf_op jit(solution)/shard_map/all_gather | solution.py:79
  15.6 220.1 %all-gather.48.cloned.1.call-start = ((), (), s32[]{:S(2)}) async-start(), calls=%async_computation.6 | async-start | bytes 6488064 | tf_op jit(solution)/shard_map/all_gather | solution.py:80
  16.9 5.2 %copy-start.12 = (bf16[2,128]{1,0:T(2,128)(2,1)S(1)}, bf16[2,128]{1,0:T(2,128)(2,1)}, u32[]{:S(2)}) copy-start(bf16[2,128]{1,0:T(2,128)(2,1)} %param.17) | copy-start | bytes 1540
  16.9 17.6 %copy-start.14 = (bf16[2,32,2]{1,2,0:T(2,128)(2,1)S(1)}, bf16[2,32,2]{1,2,0:T(2,128)(2,1)}, u32[]{:S(2)}) copy-start(bf16[2,32,2]{1,2,0:T(2,128)(2,1)} %param.22) | copy-start | bytes 772
  17.0 232.3 %all-gather.52.cloned.1.call-start = ((), (), s32[]{:S(2)}) async-start(), calls=%async_computation.8 | async-start | bytes 2359296 | tf_op jit(solution)/shard_map/all_gather | solution.py:70
  17.8 257.3 %all-gather.54.cloned.1.call-start = ((), (), s32[]{:S(2)}) async-start(), calls=%async_computation.9 | async-start | bytes 2359296 | tf_op jit(solution)/shard_map/all_gather | solution.py:71
  18.6 282.2 %all-gather.50.cloned.1.call-start = ((), (), s32[]{:S(2)}) async-start(), calls=%async_computation.7 | async-start | bytes 2359296 | tf_op jit(solution)/shard_map/all_gather | solution.py:72
  19.2 306.0 %all-gather.56.cloned.1.call-start = ((), (), s32[]{:S(2)}) async-start(), calls=%async_computation.10 | async-start | bytes 2359296 | tf_op jit(solution)/shard_map/all_gather | solution.py:73
  20.0 342.6 %all-gather.58.cloned.1.call-start = ((), (), s32[]{:S(2)}) async-start(), calls=%async_computation.11 | async-start | bytes 6488064 | tf_op jit(solution)/shard_map/all_gather | solution.py:78
  20.7 379.0 %all-gather.60.cloned.1.call-start = ((), (), s32[]{:S(2)}) async-start(), calls=%async_computation.12 | async-start | bytes 6488064 | tf_op jit(solution)/shard_map/all_gather | solution.py:79
  21.5 415.0 %all-gather.62.cloned.1.call-start = ((), (), s32[]{:S(2)}) async-start(), calls=%async_computation.13 | async-start | bytes 6488064 | tf_op jit(solution)/shard_map/all_gather | solution.py:80
  100.8 7.4 %copy-start.13 = (bf16[2,128]{1,0:T(2,128)(2,1)S(1)}, bf16[2,128]{1,0:T(2,128)(2,1)}, u32[]{:S(2)}) copy-start(bf16[2,128]{1,0:T(2,128)(2,1)} %param.23) | copy-start | bytes 1540
  194.6 15.4 %copy-start.15 = (bf16[128]{0:T(256)(128)(2,1)S(1)}, bf16[128]{0:T(256)(128)(2,1)}, u32[]{:S(2)}) copy-start(bf16[128]{0:T(256)(128)(2,1)} %param.27) | copy-start | bytes 772
  194.6 25.8 %copy-start = (bf16[1,128,1024]{2,1,0:T(8,128)(2,1)S(1)}, bf16[1,128,1024]{2,1,0:T(8,128)(2,1)}, u32[]{:S(2)}) copy-start(bf16[1,128,1024]{2,1,0:T(8,128)(2,1)} %param.15) | copy-start | bytes 786436
  220.5 7.0 %copy-start.10 = (pred[128]{0:T(512)(128)(4,1)}, pred[128]{0:T(512)(128)(4,1)S(1)}, u32[]{:S(2)}) copy-start(pred[128]{0:T(512)(128)(4,1)S(1)} %iota_compare_fusion) | copy-start | bytes 388
  228.5 2.2 copy-start.9
  235.6 7.3 %copy-start.8 = (f32[1,1024]{1,0:T(1,128)S(1)}, f32[1,1024]{1,0:T(1,128)}, u32[]{:S(2)}) copy-start(f32[1,1024]{1,0:T(1,128)} %convert_element_type.132) | copy-start | bytes 12292
  277.1 25.8 %copy-start.11 = (pred[128]{0:T(512)(128)(4,1)S(1)}, pred[128]{0:T(512)(128)(4,1)}, u32[]{:S(2)}) copy-start(pred[128]{0:T(512)(128)(4,1)} %copy-done.10) | copy-start | bytes 388
  303.9 58.7 %copy-start.7 = (f32[1,1024]{1,0:T(1,128)S(1)}, f32[1,1024]{1,0:T(1,128)}, u32[]{:S(2)}) copy-start(f32[1,1024]{1,0:T(1,128)} %convert_element_type.133) | copy-start | bytes 12292
  367.5 76.2 %copy-start.6 = (f32[8,1,128]{2,1,0:T(1,128)S(1)}, f32[8,1,128]{2,1,0:T(1,128)}, u32[]{:S(2)}) copy-start(f32[8,1,128]{2,1,0:T(1,128)} %convert_element_type.134) | copy-start | bytes 12292
Sparse Core Ops, SparseCore 0:
  8.9 27.8 all-gather.37
  38.4 24.1 all-gather.39
  64.2 24.1 all-gather.35
  90.0 22.8 all-gather.41
  114.3 35.9 all-gather.43
  151.7 35.3 all-gather.45
  188.7 35.4 all-gather.47
  225.8 23.3 all-gather.51
  250.8 24.1 all-gather.53
  276.5 24.1 all-gather.49
  302.4 22.8 all-gather.55
  326.7 35.8 all-gather.57
  364.2 35.3 all-gather.59
  401.1 35.3 all-gather.61
where the time goes:
time: 452 us; the launch traced here: 451 us
  waiting for transfers between devices  184 us (41%)
  local copies, waits for them, and re-layouts  139 us (31%)
  blocking collectives  66 us (15%)
  matrix products  42.5 us (9%)
  between operations  14.4 us (3%)
    gather x4, local copies, waits for them, and re-layouts, attention_block(): pos_bias = jnp.take(bias_table.T, buckets, axis=1).astype(jnp.float32)  129 us
    all_gather x2, waiting for transfers between devices, local_forward(): wout_full = lax.all_gather(w_out[layer_idx], 'fsdp', axis=0, tiled=True)  36.9 us
    all_gather x2, waiting for transfers between devices, local_forward(): wi0_full = lax.all_gather(w_in0[layer_idx], 'fsdp', axis=1, tiled=True)  35.2 us
    all_gather x2, waiting for transfers between devices, local_forward(): wi1_full = lax.all_gather(w_in1[layer_idx], 'fsdp', axis=1, tiled=True)  32.1 us
    all_gather x2, waiting for transfers between devices, local_forward(): wk_full = lax.all_gather(w_k[layer_idx], 'fsdp', axis=1, tiled=True)  23.6 us
    all_gather x2, waiting for transfers between devices, local_forward(): wv_full = lax.all_gather(w_v[layer_idx], 'fsdp', axis=1, tiled=True)  23.5 us
    all_gather x2, waiting for transfers between devices, local_forward(): wo_full = lax.all_gather(w_o[layer_idx], 'fsdp', axis=0, tiled=True)  21.3 us
    all_gather x2, blocking collectives, local_forward(): gain_full = lax.all_gather(attn_gain[layer_idx], 'fsdp', axis=0, tiled=True)  20.6 us
  transfers between devices with their start and end apart: 14, of which 7 were waited for; matrix products, arithmetic and copies ran while one was open for 39% of the time, Pallas kernels for 0%

commit v1 on v0

v1 whole, which is shorter than its diff:
```python
import functools

import jax
import jax.numpy as jnp
from jax import lax
from jax.experimental import pallas as pl
from jax.experimental.pallas import tpu as pltpu
from jax.sharding import PartitionSpec as P

HEAD_DIM = 64
NUM_BUCKETS = 32
NORM_EPS = 1e-6
LANES = 128
MASKED = -1e30
MESH = pl.DeviceIdType.MESH
BF16 = jnp.bfloat16
F32 = jnp.float32

ROW_ATTN, ROW_FFN, ROW_FINAL, ROW_BIAS, ROW_LEN, SMALL_ROWS = 0, 2, 4, 5, 9, 16

OWN, RT, LT, OP = 0, 1, 2, 3
TO_RIGHT = {OWN: LT, RT: OWN, LT: OP, OP: RT}
TO_LEFT = {OWN: RT, RT: OP, LT: OWN, OP: LT}


def bucket_of(rel_pos):
    half_buckets = NUM_BUCKETS // 2
    max_exact = half_buckets // 2
    distance = jnp.abs(rel_pos)
    log_bucket = jnp.full_like(distance, max_exact)
    for step in range(1, half_buckets - max_exact):
        log_bucket += jnp.where(distance * distance >= max_exact * max_exact * 2**step, 1, 0)
    return jnp.where(rel_pos > 0, half_buckets, 0) + jnp.where(distance < max_exact, distance, log_bucket)


def dot(a, b):
    return jnp.dot(a, b, preferred_element_type=F32)


def kernel(n, smalls, tok, wq, wk, wv, wo, win0, win1, wout, out,
           sm_all, gainb, lenb, biasb, tokb, nb, mb, wqkvb, wob, winb, woutb, qb, kb, vb, cb, c1b, hb, pb,
           relay_a, relay_b, recv_l, recv_r, send_sem, recv_sem, load_sem):
    seq, d_model = tok.shape[1], tok.shape[2]
    layers = wq.shape[0]
    half, rows_half = d_model // 2, seq // 2
    share = wq.shape[2]
    chip_cols = 2 * share

    me = lax.axis_index("fsdp")
    right, left = lax.rem(me + 2, n), lax.rem(me + n - 2, n)
    opposite = lax.rem(me + n // 2, n)
    partner = me + 1 - 2 * lax.rem(me, 2)
    counts = {"remote": 0, "local": 0}
    sent, done = [], set()

    def remote(src, dst, device):
        index = counts["remote"]
        counts["remote"] += 1
        copy = pltpu.make_async_remote_copy(
            src_ref=src, dst_ref=dst, send_sem=send_sem.at[index], recv_sem=recv_sem.at[index],
            device_id={"fsdp": device}, device_id_type=MESH)
        sent.append(copy)
        return copy

    def load(src, dst):
        index = counts["local"]
        counts["local"] += 1
        copy = pltpu.make_async_copy(src, dst, load_sem.at[index])
        copy.start()
        return copy

    def rows(slot, count=1):
        return pl.ds(slot * seq, count * seq)

    def part(ref, slot, r, c):
        row = pl.ds(slot * seq, seq) if r is None else pl.ds(slot * seq + r * rows_half, rows_half)
        col = slice(None) if c is None else pl.ds(c * half, half)
        return ref.at[row, col]

    tok_load = load(tok.at[0], tokb.at[rows(OWN), :])
    qkv_loads = []
    for layer in range(layers):
        qkv_loads.append([load(w.at[layer], wqkvb.at[layer, :, pl.ds(i * chip_cols, share)])
                          for i, w in enumerate((wq, wk, wv))])
        if layer == 0:
            wo_loads = [load(wo.at[k], wob.at[k, OWN, pl.ds(0, share), :]) for k in range(layers)]
            in_loads = []
            out_loads = []
        in_loads.append([load(w.at[layer], winb.at[layer, i, 0]) for i, w in enumerate((win0, win1))])
        out_loads.append(load(wout.at[layer], woutb.at[layer, 0]))

    barrier = pltpu.get_barrier_semaphore()
    for k in range(1, n):
        pl.semaphore_signal(barrier, inc=1, device_id={"fsdp": lax.rem(me + k, n)}, device_id_type=MESH)
    pl.semaphore_wait(barrier, n - 1)

    def block_sends(src, dst):
        to_right = [remote(src(c), dst(LT, c), right) for c in range(2)]
        to_left = [remote(src(c), dst(RT, c), left) for c in range(2)]
        return to_right, to_left

    def block_forwards(dst):
        return remote(dst(LT, 0), dst(OP, 0), right), remote(dst(RT, 1), dst(OP, 1), left)

    small_sends = [remote(smalls, sm_all.at[me], lax.rem(me + k, n)) for k in range(1, n)]
    tok_src = lambda c: tok.at[0, :, pl.ds(c * half, half)]
    tok_dst = lambda slot, c: part(tokb, slot, None, c)
    tok_r, tok_l = block_sends(tok_src, tok_dst)
    qkv_push = [[remote(w.at[layer], wqkvb.at[layer, :, pl.ds(i * chip_cols + share, share)], partner)
                 for i, w in enumerate((wq, wk, wv))] for layer in range(layers)]
    in_push = [[remote(w.at[layer], winb.at[layer, i, 1], partner) for i, w in enumerate((win0, win1))]
               for layer in range(layers)]
    out_push = [remote(wout.at[layer], woutb.at[layer, 1], partner) for layer in range(layers)]
    wo_push = [remote(wo.at[layer], wob.at[layer, OWN, pl.ds(share, share), :], partner) for layer in range(layers)]

    for copy in small_sends:
        copy.start()
    tok_r[0].start()
    tok_l[1].start()
    tok_r[1].start()
    tok_l[0].start()
    for copy in qkv_push[0]:
        copy.start()
    wo_push[0].start()

    sm_all[me] = smalls[...]
    for copy in small_sends:
        copy.wait_recv()
    for k in range(n):
        gainb[:, k * LANES:(k + 1) * LANES] = sm_all[k, 0:8, :]
    for slot, device in ((OWN, me), (RT, right), (LT, left), (OP, opposite)):
        lenb[slot] = jnp.broadcast_to(sm_all[device, ROW_LEN:ROW_LEN + 1, :], (8, LANES))

    def norm_rows(load_row, gain_row, dst, start, count):
        step = 32

        def body(i, carry):
            r = pl.multiple_of(start + i * step, step)
            x = load_row(r, step)
            mean_sq = jnp.mean(x * x, axis=-1, keepdims=True)
            normed = x * lax.rsqrt(mean_sq + NORM_EPS) * gainb[gain_row:gain_row + 1, :]
            dst[pl.ds(r, step), :] = normed.astype(BF16)
            return carry

        lax.fori_loop(0, count // step, body, 0)

    def token_row(r, step):
        return tokb[pl.ds(r, step), :].astype(F32)

    def hidden_row(r, step):
        return hb[pl.ds(r, step), :]

    lane_low = lax.rem(lax.broadcasted_iota(jnp.int32, (1, chip_cols), 1), 2 * HEAD_DIM) < HEAD_DIM

    def project(layer, src, slot, count):
        x = src[rows(slot, count), :]
        q = dot(x, wqkvb[layer, :, 0:chip_cols])
        qb[rows(slot, count), :] = q.astype(BF16)
        for i, ref in ((1, kb), (2, vb)):
            y = dot(x, wqkvb[layer, :, i * chip_cols:(i + 1) * chip_cols])
            ref[0, rows(slot, count), :] = jnp.where(lane_low, y, 0.0).astype(BF16)
            ref[1, rows(slot, count), :] = jnp.where(lane_low, 0.0, y).astype(BF16)

    key_index = lax.broadcasted_iota(jnp.int32, (1, seq), 1).astype(F32)

    def attend(layer, slot, count):
        def body(i, carry):
            s = slot + i
            row = pl.ds(pl.multiple_of(s * seq, seq), seq)
            key_ok = key_index < lenb[s, 0:1, :]
            for pair in range(chip_cols // LANES):
                col = pl.ds(pair * LANES, LANES)
                keys = jnp.concatenate([kb[0, row, col], kb[1, row, col]], axis=0)
                scores = lax.dot_general(qb[row, col], keys, (((1,), (1,)), ((), ())), preferred_element_type=F32)
                scores = scores + biasb[layer, pair]
                probs = []
                for h in range(2):
                    x = jnp.where(key_ok, scores[:, h * seq:(h + 1) * seq], MASKED)
                    e = jnp.exp(x - jnp.max(x, axis=-1, keepdims=True))
                    probs.append((e / jnp.sum(e, axis=-1, keepdims=True)).astype(BF16))
                values = jnp.concatenate([vb[0, row, col], vb[1, row, col]], axis=0)
                cb[0, row, col] = dot(jnp.concatenate(probs, axis=1), values).astype(BF16)
            return carry

        lax.fori_loop(0, count, body, 0)

    def build_bias():
        rel = lax.broadcasted_iota(jnp.int32, (LANES, 2 * seq), 1)
        rel = jnp.where(rel < seq, rel, rel - 2 * seq)
        one_hot = jnp.where(bucket_of(rel) == lax.broadcasted_iota(jnp.int32, (LANES, 2 * seq), 0), 1.0, 0.0)
        one_hot = one_hot.astype(BF16)
        for pair, device in ((0, me), (1, partner)):
            table = dot(sm_all[device].astype(BF16), one_hot)
            for layer in range(layers):
                for h in range(2):
                    row = ROW_BIAS + 2 * layer + h
                    line = jnp.broadcast_to(table[row:row + 1, :], (seq, 2 * seq))
                    shifted = pltpu.roll(line, 0, 1, stride=1, stride_axis=0)
                    biasb[layer, pair, :, h * seq:(h + 1) * seq] = shifted[:, 0:seq]

    tok_load.wait()
    norm_rows(token_row, ROW_ATTN, nb, OWN * seq, seq)
    build_bias()
    for copy in qkv_loads[0]:
        copy.wait()
    for copy in qkv_push[0]:
        copy.wait_recv()
    project(0, nb, OWN, 1)
    attend(0, OWN, 1)

    tok_fr, tok_fl = block_forwards(tok_dst)
    tok_r[0].wait_recv()
    tok_fr.start()
    tok_l[1].wait_recv()
    tok_fl.start()

    def c_part(src, slot, pair):
        return cb.at[src, rows(slot), pl.ds(pair * LANES, LANES)]

    c_r, c_l = {}, {}

    def send_context(slot):
        c_r[slot] = [remote(c_part(0, slot, p), c_part(LT, TO_RIGHT[slot], p), right) for p in range(2)]
        c_l[slot] = [remote(c_part(0, slot, p), c_part(RT, TO_LEFT[slot], p), left) for p in range(2)]
        c_r[slot][0].start()
        c_l[slot][1].start()
        c_r[slot][1].start()
        c_l[slot][0].start()

    send_context(OWN)

    def wo_copies(layer):
        src = lambda c: wo.at[layer, :, pl.ds(c * half, half)]
        dst = lambda slot, c: wob.at[layer, slot, pl.ds(0, share), pl.ds(c * half, half)]
        to_right, to_left = block_sends(src, dst)
        fr, fl = block_forwards(dst)
        push = {s: remote(wob.at[layer, s, pl.ds(0, share), :], wob.at[layer, s, pl.ds(share, share), :], partner)
                for s in (RT, LT, OP)}
        return to_right, to_left, fr, fl, push

    wo_r, wo_l, wo_fr, wo_fl, wo_share = zip(*[wo_copies(layer) for layer in range(layers)])

    def start_wo(layer):
        wo_r[layer][0].start()
        wo_l[layer][1].start()
        wo_r[layer][1].start()
        wo_l[layer][0].start()

    def forward_wo(layer):
        wo_r[layer][0].wait_recv()
        wo_fr[layer].start()
        wo_l[layer][1].wait_recv()
        wo_fl[layer].start()

    def share_wo_near(layer):
        wo_r[layer][1].wait_recv()
        wo_share[layer][LT].start()
        wo_l[layer][0].wait_recv()
        wo_share[layer][RT].start()

    def share_wo_far(layer):
        wo_fr[layer].wait_recv()
        wo_fl[layer].wait_recv()
        wo_share[layer][OP].start()

    start_wo(0)
    for copy in in_push[0]:
        copy.start()
    out_push[0].start()

    tok_r[1].wait_recv()
    tok_l[0].wait_recv()
    norm_rows(token_row, ROW_ATTN, nb, RT * seq, 2 * seq)
    project(0, nb, RT, 2)
    attend(0, RT, 2)
    send_context(RT)
    send_context(LT)

    tok_fr.wait_recv()
    tok_fl.wait_recv()
    norm_rows(token_row, ROW_ATTN, nb, OP * seq, seq)
    project(0, nb, OP, 1)
    attend(0, OP, 1)
    forward_wo(0)
    send_context(OP)

    def add_context(layer, src, slot, count, first):
        for j in range(0, d_model, chip_cols):
            col = pl.ds(j, chip_cols)
            y = dot(cb[src, rows(slot, count), :], wob[layer, src, :, col])
            if first:
                hb[rows(slot, count), col] = tokb[rows(slot, count), col].astype(F32) + y
            else:
                hb[rows(slot, count), col] += y

    c_fr, c_fl = {}, {}

    def forward_context(slot):
        near, far = TO_RIGHT[slot], TO_RIGHT[TO_RIGHT[slot]]
        c_fr[slot] = remote(c_part(LT, near, 0), c_part(OP, far, 0), right)
        c_r[slot][0].wait_recv()
        c_fr[slot].start()
        near, far = TO_LEFT[slot], TO_LEFT[TO_LEFT[slot]]
        c_fl[slot] = remote(c_part(RT, near, 1), c_part(OP, far, 1), left)
        c_l[slot][1].wait_recv()
        c_fl[slot].start()

    forward_context(OWN)
    wo_loads[0].wait()
    wo_push[0].wait_recv()
    add_context(0, OWN, OWN, 4, True)
    share_wo_near(0)
    forward_context(RT)
    forward_context(LT)
    share_wo_far(0)
    forward_context(OP)
    for slot in (OWN, RT, LT, OP):
        c_r[slot][1].wait_recv()
        c_l[slot][0].wait_recv()
    for slot in (RT, LT, OP):
        wo_share[0][slot].wait_recv()
    start_wo(1)
    add_context(0, LT, OWN, 4, False)
    add_context(0, RT, OWN, 4, False)
    for copy in in_loads[0]:
        copy.wait()
    out_loads[0].wait()
    for copy in in_push[0]:
        copy.wait_recv()
    out_push[0].wait_recv()

    def feed_forward(layer, slot, count):
        x = mb[layer, rows(slot, count), :]
        mixed = []
        for i in range(2):
            gate = dot(x, winb[layer, 0, i])
            lin = dot(x, winb[layer, 1, i])
            mixed.append((jax.nn.gelu(gate, approximate=True) * lin).astype(BF16))
        for j in range(0, d_model, chip_cols):
            col = pl.ds(j, chip_cols)
            pb[layer, rows(slot, count), col] = (
                dot(mixed[0], woutb[layer, 0, :, col]) + dot(mixed[1], woutb[layer, 1, :, col]))

    def scatter_copies(layer):
        p, ra, rb = pb.at[layer], relay_a.at[layer], relay_b.at[layer]
        rl, rr = recv_l.at[layer], recv_r.at[layer]
        row = lambda r: pl.ds(r * rows_half, rows_half)
        copies = {}
        for r in range(2):
            copies["op_r", r] = remote(part(p, OP, r, 0), ra.at[row(r), :], right)
            copies["op_l", r] = remote(part(p, OP, r, 1), rb.at[row(r), :], left)
            copies["plain_r", r] = remote(part(p, RT, r, 1), part(rl, 0, r, 1), right)
            copies["plain_l", r] = remote(part(p, LT, r, 0), part(rr, 0, r, 0), left)
            copies["sum_r", r] = remote(part(p, RT, r, 0), part(rl, 0, r, 0), right)
            copies["sum_l", r] = remote(part(p, LT, r, 1), part(rr, 0, r, 1), left)
        return copies

    def pass_on(layer, copies, r):
        a = pl.ds(RT * seq + r * rows_half, rows_half)
        b = pl.ds(LT * seq + r * rows_half, rows_half)
        row = pl.ds(r * rows_half, rows_half)
        copies["op_r", r].wait_recv()
        pb[layer, a, 0:half] += relay_a[layer, row, :]
        copies["sum_r", r].start()
        copies["op_l", r].wait_recv()
        pb[layer, b, half:d_model] += relay_b[layer, row, :]
        copies["sum_l", r].start()

    def collect(layer, copies, r):
        for name in ("plain_r", "plain_l", "sum_r", "sum_l"):
            copies[name, r].wait_recv()
        row = pl.ds(r * rows_half, rows_half)
        hb[row, :] = hb[row, :] + ((pb[layer, row, :] + recv_l[layer, row, :]) + recv_r[layer, row, :])

    rs = scatter_copies(0)
    for slot in (OWN, RT, LT, OP):
        c_fr[slot].wait_recv()
        c_fl[slot].wait_recv()
    add_context(0, OP, OP, 1, False)
    norm_rows(hidden_row, ROW_FFN, mb.at[0], OP * seq, seq)
    feed_forward(0, OP, 1)
    for r in range(2):
        rs["op_r", r].start()
        rs["op_l", r].start()
    add_context(0, OP, OWN, 3, False)
    norm_rows(hidden_row, ROW_FFN, mb.at[0], OWN * seq, 3 * seq)
    feed_forward(0, RT, 2)
    rs["plain_r", 0].start()
    rs["plain_l", 0].start()
    feed_forward(0, OWN, 1)
    pass_on(0, rs, 0)
    rs["plain_r", 1].start()
    rs["plain_l", 1].start()
    pass_on(0, rs, 1)
    for copy in qkv_push[1]:
        copy.start()
    wo_push[1].start()
    for copy in in_push[1]:
        copy.start()
    out_push[1].start()

    def gather_copies(ref, r):
        to_right = [remote(part(ref, OWN, r, c), part(ref, LT, r, c), right) for c in range(2)]
        to_left = [remote(part(ref, OWN, r, c), part(ref, RT, r, c), left) for c in range(2)]
        fr = remote(part(ref, LT, r, 0), part(ref, OP, r, 0), right)
        fl = remote(part(ref, RT, r, 1), part(ref, OP, r, 1), left)
        return to_right, to_left, fr, fl

    n_gather = [gather_copies(mb.at[2], r) for r in range(2)]
    for r in range(2):
        collect(0, rs, r)
        norm_rows(hidden_row, 1, mb.at[2], r * rows_half, rows_half)
        to_right, to_left, _, _ = n_gather[r]
        to_right[0].start()
        to_left[1].start()
        to_right[1].start()
        to_left[0].start()

    def forward_gather(gather):
        to_right, to_left, fr, fl = gather
        to_right[0].wait_recv()
        fr.start()
        to_left[1].wait_recv()
        fl.start()

    forward_gather(n_gather[0])
    for copy in qkv_loads[1]:
        copy.wait()
    for copy in qkv_push[1]:
        copy.wait_recv()
    for copies in c_r, c_l:
        for slot in (OWN, RT, LT, OP):
            for copy in copies[slot]:
                copy.wait_send()
                done.add(id(copy))
    project(1, mb.at[2], OWN, 1)
    attend(1, OWN, 1)
    forward_gather(n_gather[1])
    forward_wo(1)
    share_wo_near(1)
    for r in range(2):
        n_gather[r][0][1].wait_recv()
        n_gather[r][1][0].wait_recv()
    project(1, mb.at[2], RT, 2)
    attend(1, RT, 2)
    ctx_r = remote(cb.at[0, rows(RT), :], c1b.at[LT], right)
    ctx_l = remote(cb.at[0, rows(LT), :], c1b.at[RT], left)
    ctx_o = remote(cb.at[0, rows(OP), :], c1b.at[OP], opposite)
    ctx_r.start()
    ctx_l.start()
    for r in range(2):
        n_gather[r][2].wait_recv()
        n_gather[r][3].wait_recv()
    project(1, mb.at[2], OP, 1)
    attend(1, OP, 1)
    ctx_o.start()
    share_wo_far(1)
    wo_loads[1].wait()
    wo_push[1].wait_recv()

    def add_second(src, context):
        for j in range(0, d_model, chip_cols):
            col = pl.ds(j, chip_cols)
            hb[rows(OWN), col] += dot(context, wob[1, src, :, col])

    add_second(OWN, cb[0, rows(OWN), :])
    for slot, copy in ((LT, ctx_r), (RT, ctx_l), (OP, ctx_o)):
        wo_share[1][slot].wait_recv()
        copy.wait_recv()
        add_second(slot, c1b[slot])
    norm_rows(hidden_row, ROW_FFN + 1, mb.at[1], OWN * seq, seq)
    m_gather = [gather_copies(mb.at[1], r) for r in range(2)]
    for first, second in ((0, 1), (1, 0)):
        for r in range(2):
            m_gather[r][0][first].start()
            m_gather[r][1][second].start()
    for copy in in_loads[1]:
        copy.wait()
    out_loads[1].wait()
    for copy in in_push[1]:
        copy.wait_recv()
    out_push[1].wait_recv()
    rs = scatter_copies(1)
    feed_forward(1, OWN, 1)
    for r in range(2):
        forward_gather(m_gather[r])
    for r in range(2):
        m_gather[r][0][1].wait_recv()
        m_gather[r][1][0].wait_recv()
    feed_forward(1, RT, 2)
    rs["plain_r", 0].start()
    rs["plain_l", 0].start()
    for r in range(2):
        m_gather[r][2].wait_recv()
        m_gather[r][3].wait_recv()
    feed_forward(1, OP, 1)
    for r in range(2):
        rs["op_r", r].start()
        rs["op_l", r].start()
    rs["plain_r", 1].start()
    rs["plain_l", 1].start()
    for r in range(2):
        pass_on(1, rs, r)
    for r in range(2):
        collect(1, rs, r)
        norm_rows(hidden_row, ROW_FINAL, out, r * rows_half, rows_half)
    for copy in sent:
        if id(copy) not in done:
            copy.wait_send()


def encode(n, smalls, tokens, w_q, w_k, w_v, w_o, w_in0, w_in1, w_out):
    _, seq, d_model = tokens.shape
    layers, _, share = w_q.shape
    ff_share = w_in0.shape[2]
    chip_cols = 2 * share
    ring = n // 2
    any_spec = pl.BlockSpec(memory_space=pl.ANY)
    vmem = pl.BlockSpec(memory_space=pltpu.VMEM)
    scratch = [
        pltpu.VMEM((n, SMALL_ROWS, LANES), F32),
        pltpu.VMEM((8, d_model), F32),
        pltpu.VMEM((ring, 8, LANES), F32),
        pltpu.VMEM((layers, 2, seq, 2 * seq), F32),
        pltpu.VMEM((ring * seq, d_model), BF16),
        pltpu.VMEM((ring * seq, d_model), BF16),
        pltpu.VMEM((layers + 1, ring * seq, d_model), BF16),
        pltpu.VMEM((layers, d_model, 3 * chip_cols), BF16),
        pltpu.VMEM((layers, ring, chip_cols, d_model), BF16),
        pltpu.VMEM((layers, 2, 2, d_model, ff_share), BF16),
        pltpu.VMEM((layers, 2, ff_share, d_model), BF16),
        pltpu.VMEM((ring * seq, chip_cols), BF16),
        pltpu.VMEM((2, ring * seq, chip_cols), BF16),
        pltpu.VMEM((2, ring * seq, chip_cols), BF16),
        pltpu.VMEM((ring, ring * seq, chip_cols), BF16),
        pltpu.VMEM((ring, seq, chip_cols), BF16),
        pltpu.VMEM((ring * seq, d_model), F32),
        pltpu.VMEM((layers, ring * seq, d_model), F32),
        pltpu.VMEM((layers, seq, d_model // 2), F32),
        pltpu.VMEM((layers, seq, d_model // 2), F32),
        pltpu.VMEM((layers, seq, d_model), F32),
        pltpu.VMEM((layers, seq, d_model), F32),
        pltpu.SemaphoreType.DMA((160,)),
        pltpu.SemaphoreType.DMA((160,)),
        pltpu.SemaphoreType.DMA((24,)),
    ]
    return pl.pallas_call(
        functools.partial(kernel, n),
        out_shape=jax.ShapeDtypeStruct((seq, d_model), BF16),
        in_specs=[vmem] + [any_spec] * 8,
        out_specs=vmem,
        scratch_shapes=scratch,
        compiler_params=pltpu.CompilerParams(
            collective_id=0, has_side_effects=True, vmem_limit_bytes=56 * 1024 * 1024),
    )(smalls, tokens, w_q, w_k, w_v, w_o, w_in0, w_in1, w_out)


def solution(mesh):
    n = mesh.shape["fsdp"]
    batch_spec = P(("dp", "fsdp"))
    col_spec = P(None, None, "fsdp")
    row_spec = P(None, "fsdp", None)
    gain_spec = P(None, "fsdp")
    in_specs = (batch_spec, batch_spec, gain_spec, col_spec, col_spec, col_spec, row_spec, col_spec, gain_spec,
                col_spec, col_spec, row_spec, P("fsdp"))

    def local_forward(tokens, lengths, attn_gain, w_q, w_k, w_v, w_o, rel_bias, ffn_gain, w_in0, w_in1, w_out, final_gain):
        seq_len = tokens.shape[1]
        layers, buckets, heads = rel_bias.shape
        bias_rows = jnp.pad(jnp.swapaxes(rel_bias, 1, 2).reshape(layers * heads, buckets), ((0, 0), (0, LANES - buckets)))
        length_row = jnp.broadcast_to(lengths.astype(F32)[:, None], (1, LANES))
        smalls = jnp.concatenate(
            [attn_gain.astype(F32), ffn_gain.astype(F32), final_gain.astype(F32)[None], bias_rows.astype(F32), length_row], axis=0)
        smalls = jnp.pad(smalls, ((0, SMALL_ROWS - smalls.shape[0]), (0, 0)))
        normed_out = encode(n, smalls, tokens, w_q, w_k, w_v, w_o, w_in0, w_in1, w_out)
        key_ok = jnp.arange(seq_len, dtype=jnp.int32)[:, None] < lengths
        return jnp.where(key_ok, normed_out, jnp.zeros_like(normed_out))[None]

    return jax.shard_map(local_forward, mesh=mesh, in_specs=in_specs, out_specs=batch_spec, check_vma=False)
```

time: 452 us -> 112 us (0.25)
  waiting for transfers between devices: 184 us -> 0 us
  local copies, waits for them, and re-layouts: 139 us -> 5.63 us
  Pallas kernels: 0 us -> 101 us
  blocking collectives: 66 us -> 0 us
  matrix products: 42.5 us -> 0 us
  between operations: 14.4 us -> 0.67 us
    all_gather x14 -> x0, waiting for transfers between devices: 179 us -> none  [the longest x2 36.9 us: local_forward(): wout_full = lax.all_gather(w_out[layer_idx], 'fsdp', axis=0, tiled=True)]
    gather x4 -> x0, local copies, waits for them, and re-layouts: 129 us -> none  [attention_block(): pos_bias = jnp.take(bias_table.T, buckets, axis=1).astype(jnp.float32)]
    pallas_call x0 -> x1, Pallas kernels: none -> 101 us  [encode(): pl.pallas_call(functools.partial(kernel, n), out_shape=jax.ShapeDtypeStru...]
    all_gather x7 -> x0, blocking collectives: 66 us -> none  [the longest x2 20.6 us: local_forward(): gain_full = lax.all_gather(attn_gain[layer_idx], 'fsdp', axis=0, tiled=True)]
    dot_general x16 -> x0, matrix products: 42.5 us -> none  [the longest x2 14.5 us: ffn_block(): jnp.einsum('bsf,fd->bsd', mixed_act, w_out, preferred_element_type=jnp.fl...]
    slice x10 -> x0, local copies, waits for them, and re-layouts: 9.27 us -> none  [the longest x1 1.96 us: local_forward(): wq_full = lax.all_gather(w_q[layer_idx], 'fsdp', axis=1, tiled=True)]
    unnamed x14 -> x0, waiting for transfers between devices: 4.97 us -> none
  transfers between devices with their start and end apart: 14 -> 0, of which waited for: 7 -> 0; matrix products, arithmetic and copies ran while one was open for 39% -> 0% of each run, Pallas kernels for 0% -> 0%
where the time goes in v1:
time: 112 us; the launch traced here: 110 us
  Pallas kernels  101 us (90%)
  local copies, waits for them, and re-layouts  5.63 us (5%)
  other arithmetic  3.09 us (3%)
    pallas_call x1, Pallas kernels, encode(): pl.pallas_call(functools.partial(kernel, n), out_shape=jax.ShapeDtypeStru...  101 us
    unnamed x4, local copies, waits for them, and re-layouts  4.26 us

profile of v1, /device:TPU:81, one launch (start us, length us, event | category | flops | bytes accessed | tf_op | source)
XLA Modules:
  0.0 109.9 jit_solution(17965105387506744498)
XLA Ops:
  0.7 0.7 bitcast_convert_fusion
  1.3 0.7 pad_convert_fusion
  2.0 0.8 concatenate.3
  2.8 0.6 pad.9.smalls
  3.4 0.0 copy-start
  3.4 2.7 %copy.14.win0 = bf16[2,1024,352]{2,1,0:T(8,128)(2,1)} copy(bf16[2,1024,352]{1,2,0:T(8,128)(2,1)} %param.22) | data formatting | bytes 2883584 | tf_op args[9]
  6.1 0.0 copy-done
  6.1 1.6 %copy.15.win1 = bf16[2,1024,352]{2,1,0:T(8,128)(2,1)} copy(bf16[2,1024,352]{1,2,0:T(8,128)(2,1)S(1)} %copy-done) | data formatting | bytes 2883584 | tf_op args[10]
  7.6 100.5 %shard_map.127 = bf16[128,1024]{1,0:T(8,128)(2,1)} custom-call(f32[16,128]{1,0:T(8,128)} %pad.9.smalls, bf16[1,128,1024]{2,1,0:T(8,128)(2,1)} %tok.1, bf16[2,1024,128]{2,1,0:T(8,128)(2,1)} %wq.1, bf16[2,1024,128]{2,1,0:T(8,128)(2,1)} %wk.1, bf16[2,1024,128]{2,1,0:T(8,128)(2,1)} %wv.1, bf16[2,128,1024]{2,1,0:T(8,128)(2,1)} %wo.1, ...), custom_call_target="tpu_custom_call" | custom-call | tf_op jit(solution)/shard_map/pallas_call | solution.py:547
  108.2 1.7 %select_bitcast_fusion = bf16[1,128,1024]{2,1,0:T(8,128)(2,1)} fusion(bf16[128,1024]{1,0:T(8,128)(2,1)} %shard_map.127, pred[128]{0:T(512)(128)(4,1)S(1)} %iota_compare_fusion), kind=kLoop, calls=%fused_computation | loop fusion | flops 131072 | bytes 524416 | tf_op jit(solution)/shard_map/broadcast_in_dim | solution.py:577
  (2 shorter events, 0.0 us)
Async XLA Ops:
  3.4 2.7 %copy-start = (bf16[2,1024,352]{1,2,0:T(8,128)(2,1)S(1)}, bf16[2,1024,352]{1,2,0:T(8,128)(2,1)}, u32[]{:S(2)}) copy-start(bf16[2,1024,352]{1,2,0:T(8,128)(2,1)} %param.23) | copy-start | bytes 4325380

commit v2 on v1

--- a/solution.py
+++ b/solution.py
@@ -16,7 +16,7 @@
 BF16 = jnp.bfloat16
 F32 = jnp.float32
 
-ROW_ATTN, ROW_FFN, ROW_FINAL, ROW_BIAS, ROW_LEN, SMALL_ROWS = 0, 2, 4, 5, 9, 16
+ROW_ATTN, ROW_FFN, ROW_FINAL, ROW_BIAS, ROW_LEN, SMALL_ROWS = 0, 2, 4, 5, 6, 8
 
 OWN, RT, LT, OP = 0, 1, 2, 3
 TO_RIGHT = {OWN: LT, RT: OWN, LT: OP, OP: RT}
@@ -37,13 +37,17 @@
     return jnp.dot(a, b, preferred_element_type=F32)
 
 
-def kernel(n, smalls, tok, wq, wk, wv, wo, win0, win1, wout, out,
-           sm_all, gainb, lenb, biasb, tokb, nb, mb, wqkvb, wob, winb, woutb, qb, kb, vb, cb, c1b, hb, pb,
+def dot_rows(a, b):
+    return lax.dot_general(a, b, (((1,), (1,)), ((), ())), preferred_element_type=F32)
+
+
+def kernel(n, lengths, attn_gain, ffn_gain, final_gain, bias_table, tok, wq, wk, wv, wo, win0, win1, wout, out,
+           smalls, sm_all, gainb, lenb, biasb, tokb, nb, mb, wqkvb, wob, winb, woutb, qb, kb, vb, cb, c1b, hb, pb,
            relay_a, relay_b, recv_l, recv_r, send_sem, recv_sem, load_sem):
     seq, d_model = tok.shape[1], tok.shape[2]
     layers = wq.shape[0]
     half, rows_half = d_model // 2, seq // 2
-    share = wq.shape[2]
+    share, ff_share = wq.shape[2], wout.shape[1]
     chip_cols = 2 * share
 
     me = lax.axis_index("fsdp")
@@ -86,8 +90,15 @@
             wo_loads = [load(wo.at[k], wob.at[k, OWN, pl.ds(0, share), :]) for k in range(layers)]
             in_loads = []
             out_loads = []
-        in_loads.append([load(w.at[layer], winb.at[layer, i, 0]) for i, w in enumerate((win0, win1))])
-        out_loads.append(load(wout.at[layer], woutb.at[layer, 0]))
+        in_loads.append([load(w.at[layer], winb.at[layer, i, pl.ds(0, ff_share), :]) for i, w in enumerate((win0, win1))])
+        out_loads.append(load(wout.at[layer], woutb.at[layer, pl.ds(0, ff_share), :]))
+
+    smalls[ROW_ATTN:ROW_ATTN + layers, :] = attn_gain[...].astype(F32)
+    smalls[ROW_FFN:ROW_FFN + layers, :] = ffn_gain[...].astype(F32)
+    smalls[ROW_FINAL:ROW_FINAL + 1, :] = final_gain[...].astype(F32)
+    table = bias_table[...].astype(F32)
+    smalls[ROW_BIAS:ROW_BIAS + 1, :] = jnp.concatenate([table[i:i + 1] for i in range(table.shape[0])], axis=1)
+    smalls[ROW_LEN:SMALL_ROWS, :] = jnp.full((SMALL_ROWS - ROW_LEN, LANES), lengths[0], jnp.int32).astype(F32)
 
     barrier = pltpu.get_barrier_semaphore()
     for k in range(1, n):
@@ -103,20 +114,21 @@
         return remote(dst(LT, 0), dst(OP, 0), right), remote(dst(RT, 1), dst(OP, 1), left)
 
     small_sends = [remote(smalls, sm_all.at[me], lax.rem(me + k, n)) for k in range(1, n)]
-    tok_src = lambda c: tok.at[0, :, pl.ds(c * half, half)]
+    tok_src = lambda c: part(tokb, OWN, None, c)
     tok_dst = lambda slot, c: part(tokb, slot, None, c)
     tok_r, tok_l = block_sends(tok_src, tok_dst)
     qkv_push = [[remote(w.at[layer], wqkvb.at[layer, :, pl.ds(i * chip_cols + share, share)], partner)
                  for i, w in enumerate((wq, wk, wv))] for layer in range(layers)]
-    in_push = [[remote(w.at[layer], winb.at[layer, i, 1], partner) for i, w in enumerate((win0, win1))]
+    in_push = [[remote(w.at[layer], winb.at[layer, i, pl.ds(ff_share, ff_share), :], partner) for i, w in enumerate((win0, win1))]
                for layer in range(layers)]
-    out_push = [remote(wout.at[layer], woutb.at[layer, 1], partner) for layer in range(layers)]
+    out_push = [remote(wout.at[layer], woutb.at[layer, pl.ds(ff_share, ff_share), :], partner) for layer in range(layers)]
     wo_push = [remote(wo.at[layer], wob.at[layer, OWN, pl.ds(share, share), :], partner) for layer in range(layers)]
 
+    tok_load.wait()
+    tok_r[0].start()
+    tok_l[1].start()
     for copy in small_sends:
         copy.start()
-    tok_r[0].start()
-    tok_l[1].start()
     tok_r[1].start()
     tok_l[0].start()
     for copy in qkv_push[0]:
@@ -127,7 +139,7 @@
     for copy in small_sends:
         copy.wait_recv()
     for k in range(n):
-        gainb[:, k * LANES:(k + 1) * LANES] = sm_all[k, 0:8, :]
+        gainb[:, k * LANES:(k + 1) * LANES] = sm_all[k]
     for slot, device in ((OWN, me), (RT, right), (LT, left), (OP, opposite)):
         lenb[slot] = jnp.broadcast_to(sm_all[device, ROW_LEN:ROW_LEN + 1, :], (8, LANES))
 
@@ -171,7 +183,7 @@
             for pair in range(chip_cols // LANES):
                 col = pl.ds(pair * LANES, LANES)
                 keys = jnp.concatenate([kb[0, row, col], kb[1, row, col]], axis=0)
-                scores = lax.dot_general(qb[row, col], keys, (((1,), (1,)), ((), ())), preferred_element_type=F32)
+                scores = dot_rows(qb[row, col], keys)
                 scores = scores + biasb[layer, pair]
                 probs = []
                 for h in range(2):
@@ -187,18 +199,21 @@
     def build_bias():
         rel = lax.broadcasted_iota(jnp.int32, (LANES, 2 * seq), 1)
         rel = jnp.where(rel < seq, rel, rel - 2 * seq)
-        one_hot = jnp.where(bucket_of(rel) == lax.broadcasted_iota(jnp.int32, (LANES, 2 * seq), 0), 1.0, 0.0)
-        one_hot = one_hot.astype(BF16)
+        lane = lax.broadcasted_iota(jnp.int32, (LANES, 2 * seq), 0)
+        one_hot = jnp.where(bucket_of(rel) == lax.rem(lane, NUM_BUCKETS), 1.0, 0.0).astype(BF16)
+        table_row = lax.broadcasted_iota(jnp.int32, (8, LANES), 0)
+        table_lane = lax.broadcasted_iota(jnp.int32, (8, LANES), 1)
+        own_lanes = table_row == table_lane // NUM_BUCKETS
         for pair, device in ((0, me), (1, partner)):
-            table = dot(sm_all[device].astype(BF16), one_hot)
+            tables = jnp.where(own_lanes, sm_all[device, ROW_BIAS:ROW_BIAS + 1, :], 0.0)
+            lines = dot(tables.astype(BF16), one_hot)
             for layer in range(layers):
                 for h in range(2):
-                    row = ROW_BIAS + 2 * layer + h
-                    line = jnp.broadcast_to(table[row:row + 1, :], (seq, 2 * seq))
+                    row = 2 * layer + h
+                    line = jnp.broadcast_to(lines[row:row + 1, :], (seq, 2 * seq))
                     shifted = pltpu.roll(line, 0, 1, stride=1, stride_axis=0)
                     biasb[layer, pair, :, h * seq:(h + 1) * seq] = shifted[:, 0:seq]
 
-    tok_load.wait()
     norm_rows(token_row, ROW_ATTN, nb, OWN * seq, seq)
     build_bias()
     for copy in qkv_loads[0]:
@@ -331,15 +346,12 @@
 
     def feed_forward(layer, slot, count):
         x = mb[layer, rows(slot, count), :]
-        mixed = []
-        for i in range(2):
-            gate = dot(x, winb[layer, 0, i])
-            lin = dot(x, winb[layer, 1, i])
-            mixed.append((jax.nn.gelu(gate, approximate=True) * lin).astype(BF16))
+        gate = dot_rows(x, winb[layer, 0])
+        lin = dot_rows(x, winb[layer, 1])
+        mixed = (jax.nn.gelu(gate, approximate=True) * lin).astype(BF16)
         for j in range(0, d_model, chip_cols):
             col = pl.ds(j, chip_cols)
-            pb[layer, rows(slot, count), col] = (
-                dot(mixed[0], woutb[layer, 0, :, col]) + dot(mixed[1], woutb[layer, 1, :, col]))
+            pb[layer, rows(slot, count), col] = dot(mixed, woutb[layer, :, col])
 
     def scatter_copies(layer):
         p, ra, rb = pb.at[layer], relay_a.at[layer], relay_b.at[layer]
@@ -509,15 +521,16 @@
             copy.wait_send()
 
 
-def encode(n, smalls, tokens, w_q, w_k, w_v, w_o, w_in0, w_in1, w_out):
+def encode(n, lengths, attn_gain, ffn_gain, final_gain, bias_table, tokens, w_q, w_k, w_v, w_o, w_in0, w_in1, w_out):
     _, seq, d_model = tokens.shape
     layers, _, share = w_q.shape
-    ff_share = w_in0.shape[2]
+    ff_share = w_out.shape[1]
     chip_cols = 2 * share
     ring = n // 2
     any_spec = pl.BlockSpec(memory_space=pl.ANY)
     vmem = pl.BlockSpec(memory_space=pltpu.VMEM)
     scratch = [
+        pltpu.VMEM((SMALL_ROWS, LANES), F32),
         pltpu.VMEM((n, SMALL_ROWS, LANES), F32),
         pltpu.VMEM((8, d_model), F32),
         pltpu.VMEM((ring, 8, LANES), F32),
@@ -527,8 +540,8 @@
         pltpu.VMEM((layers + 1, ring * seq, d_model), BF16),
         pltpu.VMEM((layers, d_model, 3 * chip_cols), BF16),
         pltpu.VMEM((layers, ring, chip_cols, d_model), BF16),
-        pltpu.VMEM((layers, 2, 2, d_model, ff_share), BF16),
-        pltpu.VMEM((layers, 2, ff_share, d_model), BF16),
+        pltpu.VMEM((layers, 2, 2 * ff_share, d_model), BF16),
+        pltpu.VMEM((layers, 2 * ff_share, d_model), BF16),
         pltpu.VMEM((ring * seq, chip_cols), BF16),
         pltpu.VMEM((2, ring * seq, chip_cols), BF16),
         pltpu.VMEM((2, ring * seq, chip_cols), BF16),
@@ -546,13 +559,13 @@
     ]
     return pl.pallas_call(
         functools.partial(kernel, n),
-        out_shape=jax.ShapeDtypeStruct((seq, d_model), BF16),
-        in_specs=[vmem] + [any_spec] * 8,
+        out_shape=pltpu.VMEM((seq, d_model), BF16),
+        in_specs=[pl.BlockSpec(memory_space=pltpu.SMEM)] + [vmem] * 4 + [any_spec] * 8,
         out_specs=vmem,
         scratch_shapes=scratch,
         compiler_params=pltpu.CompilerParams(
             collective_id=0, has_side_effects=True, vmem_limit_bytes=56 * 1024 * 1024),
-    )(smalls, tokens, w_q, w_k, w_v, w_o, w_in0, w_in1, w_out)
+    )(lengths, attn_gain, ffn_gain, final_gain, bias_table, tokens, w_q, w_k, w_v, w_o, w_in0, w_in1, w_out)
 
 
 def solution(mesh):
@@ -567,12 +580,9 @@
     def local_forward(tokens, lengths, attn_gain, w_q, w_k, w_v, w_o, rel_bias, ffn_gain, w_in0, w_in1, w_out, final_gain):
         seq_len = tokens.shape[1]
         layers, buckets, heads = rel_bias.shape
-        bias_rows = jnp.pad(jnp.swapaxes(rel_bias, 1, 2).reshape(layers * heads, buckets), ((0, 0), (0, LANES - buckets)))
-        length_row = jnp.broadcast_to(lengths.astype(F32)[:, None], (1, LANES))
-        smalls = jnp.concatenate(
-            [attn_gain.astype(F32), ffn_gain.astype(F32), final_gain.astype(F32)[None], bias_rows.astype(F32), length_row], axis=0)
-        smalls = jnp.pad(smalls, ((0, SMALL_ROWS - smalls.shape[0]), (0, 0)))
-        normed_out = encode(n, smalls, tokens, w_q, w_k, w_v, w_o, w_in0, w_in1, w_out)
+        bias_table = jnp.swapaxes(rel_bias, 1, 2).reshape(layers * heads, buckets)
+        normed_out = encode(n, lengths, attn_gain, ffn_gain, final_gain[None], bias_table, tokens, w_q, w_k, w_v, w_o,
+                            jnp.swapaxes(w_in0, 1, 2), jnp.swapaxes(w_in1, 1, 2), w_out)
         key_ok = jnp.arange(seq_len, dtype=jnp.int32)[:, None] < lengths
         return jnp.where(key_ok, normed_out, jnp.zeros_like(normed_out))[None]
 

time: 112 us -> 106 us (0.946)
  local copies, waits for them, and re-layouts: 5.63 us -> 0 us
  other arithmetic: 3.09 us -> 0.8 us
  Pallas kernels: 101 us -> 103 us
    unnamed x4 -> x0, local copies, waits for them, and re-layouts: 4.26 us -> none
    pallas_call x1, Pallas kernels: 101 us -> 103 us  [encode(): pl.pallas_call(functools.partial(kernel, n), out_shape=pltpu.VMEM((seq, d...]
where the time goes in v2:
time: 106 us; the launch traced here: 104 us
  Pallas kernels  103 us (97%)
    pallas_call x1, Pallas kernels, encode(): pl.pallas_call(functools.partial(kernel, n), out_shape=pltpu.VMEM((seq, d...  103 us

profile of v2, /device:TPU:81, one launch (start us, length us, event | category | flops | bytes accessed | tf_op | source)
XLA Modules:
  0.0 104.2 jit_solution(1763917636172894262)
XLA Ops:
  0.7 102.7 %shard_map.127 = bf16[128,1024]{1,0:T(8,128)(2,1)S(1)} custom-call(s32[1]{0:T(128)} %copy.14.lengths, bf16[2,128]{1,0:T(2,128)(2,1)} %attn_gain.1, bf16[2,128]{1,0:T(2,128)(2,1)} %ffn_gain.1, bf16[1,128]{1,0:T(2,128)(2,1)} %bitcast.13, bf16[4,32]{1,0:T(4,128)(2,1)} %bitcast.12, bf16[1,128,1024]{2,1,0:T(8,128)(2,1)} %tok.1, bf16[2,1024,128]{2,1,0:T(8,128)(2,1)} %wq.1, ...), custom_call_target="tpu_custom_call" | custom-call | tf_op jit(solution)/shard_map/pallas_call | solution.py:560
  103.4 0.8 select_bitcast_fusion
  (1 shorter events, 0.0 us)

commit v3 on v2

--- a/solution.py
+++ b/solution.py
@@ -41,7 +41,7 @@
     return lax.dot_general(a, b, (((1,), (1,)), ((), ())), preferred_element_type=F32)
 
 
-def kernel(n, lengths, attn_gain, ffn_gain, final_gain, bias_table, tok, wq, wk, wv, wo, win0, win1, wout, out,
+def kernel(n, groups, lengths, attn_gain, ffn_gain, final_gain, bias_table, tok, wq, wk, wv, wo, win0, win1, wout, out,
            smalls, sm_all, gainb, lenb, biasb, tokb, nb, mb, wqkvb, wob, winb, woutb, qb, kb, vb, cb, c1b, hb, pb,
            relay_a, relay_b, recv_l, recv_r, send_sem, recv_sem, load_sem):
     seq, d_model = tok.shape[1], tok.shape[2]
@@ -50,19 +50,19 @@
     share, ff_share = wq.shape[2], wout.shape[1]
     chip_cols = 2 * share
 
-    me = lax.axis_index("fsdp")
+    me, group = lax.axis_index("fsdp"), lax.axis_index("dp")
     right, left = lax.rem(me + 2, n), lax.rem(me + n - 2, n)
     opposite = lax.rem(me + n // 2, n)
     partner = me + 1 - 2 * lax.rem(me, 2)
     counts = {"remote": 0, "local": 0}
     sent, done = [], set()
 
-    def remote(src, dst, device):
+    def remote(src, dst, device, axis="fsdp"):
         index = counts["remote"]
         counts["remote"] += 1
         copy = pltpu.make_async_remote_copy(
             src_ref=src, dst_ref=dst, send_sem=send_sem.at[index], recv_sem=recv_sem.at[index],
-            device_id={"fsdp": device}, device_id_type=MESH)
+            device_id={axis: device}, device_id_type=MESH)
         sent.append(copy)
         return copy
 
@@ -103,7 +103,9 @@
     barrier = pltpu.get_barrier_semaphore()
     for k in range(1, n):
         pl.semaphore_signal(barrier, inc=1, device_id={"fsdp": lax.rem(me + k, n)}, device_id_type=MESH)
-    pl.semaphore_wait(barrier, n - 1)
+    for k in range(1, groups):
+        pl.semaphore_signal(barrier, inc=1, device_id={"dp": lax.rem(group + k, groups)}, device_id_type=MESH)
+    pl.semaphore_wait(barrier, n - 1 + groups - 1)
 
     def block_sends(src, dst):
         to_right = [remote(src(c), dst(LT, c), right) for c in range(2)]
@@ -112,6 +114,60 @@
 
     def block_forwards(dst):
         return remote(dst(LT, 0), dst(OP, 0), right), remote(dst(RT, 1), dst(OP, 1), left)
+
+    row_pieces = min(groups, share // 16)
+    col_pieces = groups // row_pieces
+    piece_rows, piece_cols = share // row_pieces, d_model // col_pieces
+    piece_row = pl.multiple_of(group // col_pieces * piece_rows, piece_rows)
+    piece_col = pl.multiple_of(lax.rem(group, col_pieces) * piece_cols, piece_cols)
+
+    def wo_copies(layer):
+        col = lambda c: pl.ds(pl.multiple_of(piece_col + c * (piece_cols // 2), LANES), piece_cols // 2)
+        src = lambda c: wo.at[layer, pl.ds(piece_row, piece_rows), col(c)]
+        dst = lambda slot, c: wob.at[layer, slot, pl.ds(piece_row, piece_rows), col(c)]
+        to_right, to_left = block_sends(src, dst)
+        fr, fl = block_forwards(dst)
+        piece = lambda slot, count: wob.at[layer, pl.ds(slot, count), pl.ds(piece_row, piece_rows), pl.ds(piece_col, piece_cols)]
+        spread = [[remote(piece(slot, count), piece(slot, count), lax.rem(group + k, groups), "dp") for k in range(1, groups)]
+                  for slot, count in ((RT, 2), (OP, 1))]
+        push = {s: remote(wob.at[layer, s, pl.ds(0, share), :], wob.at[layer, s, pl.ds(share, share), :], partner)
+                for s in (RT, LT, OP)}
+        return to_right, to_left, fr, fl, spread, push
+
+    wo_r, wo_l, wo_fr, wo_fl, wo_spread, wo_share = zip(*[wo_copies(layer) for layer in range(layers)])
+
+    def start_wo(layer):
+        wo_r[layer][0].start()
+        wo_l[layer][1].start()
+        wo_r[layer][1].start()
+        wo_l[layer][0].start()
+
+    def forward_wo(layer):
+        wo_r[layer][0].wait_recv()
+        wo_fr[layer].start()
+        wo_l[layer][1].wait_recv()
+        wo_fl[layer].start()
+        wo_r[layer][1].wait_recv()
+        wo_l[layer][0].wait_recv()
+        for copy in wo_spread[layer][0]:
+            copy.start()
+
+    def spread_far_wo(layer):
+        wo_fr[layer].wait_recv()
+        wo_fl[layer].wait_recv()
+        for copy in wo_spread[layer][1]:
+            copy.start()
+
+    def share_wo_near(layer):
+        for copy in wo_spread[layer][0]:
+            copy.wait_recv()
+        wo_share[layer][LT].start()
+        wo_share[layer][RT].start()
+
+    def share_wo_far(layer):
+        for copy in wo_spread[layer][1]:
+            copy.wait_recv()
+        wo_share[layer][OP].start()
 
     small_sends = [remote(smalls, sm_all.at[me], lax.rem(me + k, n)) for k in range(1, n)]
     tok_src = lambda c: part(tokb, OWN, None, c)
@@ -124,6 +180,7 @@
     out_push = [remote(wout.at[layer], woutb.at[layer, pl.ds(ff_share, ff_share), :], partner) for layer in range(layers)]
     wo_push = [remote(wo.at[layer], wob.at[layer, OWN, pl.ds(share, share), :], partner) for layer in range(layers)]
 
+    start_wo(0)
     tok_load.wait()
     tok_r[0].start()
     tok_l[1].start()
@@ -223,6 +280,7 @@
     project(0, nb, OWN, 1)
     attend(0, OWN, 1)
 
+    forward_wo(0)
     tok_fr, tok_fl = block_forwards(tok_dst)
     tok_r[0].wait_recv()
     tok_fr.start()
@@ -244,41 +302,6 @@
 
     send_context(OWN)
 
-    def wo_copies(layer):
-        src = lambda c: wo.at[layer, :, pl.ds(c * half, half)]
-        dst = lambda slot, c: wob.at[layer, slot, pl.ds(0, share), pl.ds(c * half, half)]
-        to_right, to_left = block_sends(src, dst)
-        fr, fl = block_forwards(dst)
-        push = {s: remote(wob.at[layer, s, pl.ds(0, share), :], wob.at[layer, s, pl.ds(share, share), :], partner)
-                for s in (RT, LT, OP)}
-        return to_right, to_left, fr, fl, push
-
-    wo_r, wo_l, wo_fr, wo_fl, wo_share = zip(*[wo_copies(layer) for layer in range(layers)])
-
-    def start_wo(layer):
-        wo_r[layer][0].start()
-        wo_l[layer][1].start()
-        wo_r[layer][1].start()
-        wo_l[layer][0].start()
-
-    def forward_wo(layer):
-        wo_r[layer][0].wait_recv()
-        wo_fr[layer].start()
-        wo_l[layer][1].wait_recv()
-        wo_fl[layer].start()
-
-    def share_wo_near(layer):
-        wo_r[layer][1].wait_recv()
-        wo_share[layer][LT].start()
-        wo_l[layer][0].wait_recv()
-        wo_share[layer][RT].start()
-
-    def share_wo_far(layer):
-        wo_fr[layer].wait_recv()
-        wo_fl[layer].wait_recv()
-        wo_share[layer][OP].start()
-
-    start_wo(0)
     for copy in in_push[0]:
         copy.start()
     out_push[0].start()
@@ -291,12 +314,12 @@
     send_context(RT)
     send_context(LT)
 
+    spread_far_wo(0)
     tok_fr.wait_recv()
     tok_fl.wait_recv()
     norm_rows(token_row, ROW_ATTN, nb, OP * seq, seq)
     project(0, nb, OP, 1)
     attend(0, OP, 1)
-    forward_wo(0)
     send_context(OP)
 
     def add_context(layer, src, slot, count, first):
@@ -324,11 +347,11 @@
     wo_loads[0].wait()
     wo_push[0].wait_recv()
     add_context(0, OWN, OWN, 4, True)
-    share_wo_near(0)
     forward_context(RT)
     forward_context(LT)
+    share_wo_near(0)
+    forward_context(OP)
     share_wo_far(0)
-    forward_context(OP)
     for slot in (OWN, RT, LT, OP):
         c_r[slot][1].wait_recv()
         c_l[slot][0].wait_recv()
@@ -399,11 +422,13 @@
     feed_forward(0, RT, 2)
     rs["plain_r", 0].start()
     rs["plain_l", 0].start()
+    forward_wo(1)
     feed_forward(0, OWN, 1)
     pass_on(0, rs, 0)
     rs["plain_r", 1].start()
     rs["plain_l", 1].start()
     pass_on(0, rs, 1)
+    spread_far_wo(1)
     for copy in qkv_push[1]:
         copy.start()
     wo_push[1].start()
@@ -448,8 +473,8 @@
     project(1, mb.at[2], OWN, 1)
     attend(1, OWN, 1)
     forward_gather(n_gather[1])
-    forward_wo(1)
     share_wo_near(1)
+    share_wo_far(1)
     for r in range(2):
         n_gather[r][0][1].wait_recv()
         n_gather[r][1][0].wait_recv()
@@ -466,7 +491,6 @@
     project(1, mb.at[2], OP, 1)
     attend(1, OP, 1)
     ctx_o.start()
-    share_wo_far(1)
     wo_loads[1].wait()
     wo_push[1].wait_recv()
 
@@ -521,7 +545,7 @@
             copy.wait_send()
 
 
-def encode(n, lengths, attn_gain, ffn_gain, final_gain, bias_table, tokens, w_q, w_k, w_v, w_o, w_in0, w_in1, w_out):
+def encode(n, groups, lengths, attn_gain, ffn_gain, final_gain, bias_table, tokens, w_q, w_k, w_v, w_o, w_in0, w_in1, w_out):
     _, seq, d_model = tokens.shape
     layers, _, share = w_q.shape
     ff_share = w_out.shape[1]
@@ -553,12 +577,12 @@
         pltpu.VMEM((layers, seq, d_model // 2), F32),
         pltpu.VMEM((layers, seq, d_model), F32),
         pltpu.VMEM((layers, seq, d_model), F32),
-        pltpu.SemaphoreType.DMA((160,)),
-        pltpu.SemaphoreType.DMA((160,)),
+        pltpu.SemaphoreType.DMA((160 + 4 * groups,)),
+        pltpu.SemaphoreType.DMA((160 + 4 * groups,)),
         pltpu.SemaphoreType.DMA((24,)),
     ]
     return pl.pallas_call(
-        functools.partial(kernel, n),
+        functools.partial(kernel, n, groups),
         out_shape=pltpu.VMEM((seq, d_model), BF16),
         in_specs=[pl.BlockSpec(memory_space=pltpu.SMEM)] + [vmem] * 4 + [any_spec] * 8,
         out_specs=vmem,
@@ -569,7 +593,7 @@
 
 
 def solution(mesh):
-    n = mesh.shape["fsdp"]
+    n, groups = mesh.shape["fsdp"], mesh.shape["dp"]
     batch_spec = P(("dp", "fsdp"))
     col_spec = P(None, None, "fsdp")
     row_spec = P(None, "fsdp", None)
@@ -581,7 +605,7 @@
         seq_len = tokens.shape[1]
         layers, buckets, heads = rel_bias.shape
         bias_table = jnp.swapaxes(rel_bias, 1, 2).reshape(layers * heads, buckets)
-        normed_out = encode(n, lengths, attn_gain, ffn_gain, final_gain[None], bias_table, tokens, w_q, w_k, w_v, w_o,
+        normed_out = encode(n, groups, lengths, attn_gain, ffn_gain, final_gain[None], bias_table, tokens, w_q, w_k, w_v, w_o,
                             jnp.swapaxes(w_in0, 1, 2), jnp.swapaxes(w_in1, 1, 2), w_out)
         key_ok = jnp.arange(seq_len, dtype=jnp.int32)[:, None] < lengths
         return jnp.where(key_ok, normed_out, jnp.zeros_like(normed_out))[None]

time: 106 us -> 97.7 us (0.922)
  the two profiles are of different devices: /device:TPU:81 before, /device:TPU:80 now
where the time goes in v3:
time: 97.7 us; the launch traced here: 97.6 us
  Pallas kernels  96.1 us (98%)
    pallas_call x1, Pallas kernels, encode(): pl.pallas_call(functools.partial(kernel, n, groups), out_shape=pltpu.VMEM...  96.1 us

profile of v3, /device:TPU:80, one launch (start us, length us, event | category | flops | bytes accessed | tf_op | source)
XLA Modules:
  0.0 97.6 jit_solution(10938009769103258413)
XLA Ops:
  0.7 96.1 %shard_map.127 = bf16[128,1024]{1,0:T(8,128)(2,1)S(1)} custom-call(s32[1]{0:T(128)} %copy.14.lengths, bf16[2,128]{1,0:T(2,128)(2,1)} %attn_gain.1, bf16[2,128]{1,0:T(2,128)(2,1)} %ffn_gain.1, bf16[1,128]{1,0:T(2,128)(2,1)} %bitcast.13, bf16[4,32]{1,0:T(4,128)(2,1)} %bitcast.12, bf16[1,128,1024]{2,1,0:T(8,128)(2,1)} %tok.1, bf16[2,1024,128]{2,1,0:T(8,128)(2,1)} %wq.1, ...), custom_call_target="tpu_custom_call" | custom-call | tf_op jit(solution)/shard_map/pallas_call | solution.py:584
  96.8 0.8 select_bitcast_fusion
  (1 shorter events, 0.0 us)

commit v4 on v3

--- a/solution.py
+++ b/solution.py
@@ -188,6 +188,7 @@
         copy.start()
     tok_r[1].start()
     tok_l[0].start()
+    start_wo(1)
     for copy in qkv_push[0]:
         copy.start()
     wo_push[0].start()
@@ -292,44 +293,15 @@
 
     c_r, c_l = {}, {}
 
-    def send_context(slot):
+    for slot in (OWN, RT, LT, OP):
         c_r[slot] = [remote(c_part(0, slot, p), c_part(LT, TO_RIGHT[slot], p), right) for p in range(2)]
         c_l[slot] = [remote(c_part(0, slot, p), c_part(RT, TO_LEFT[slot], p), left) for p in range(2)]
-        c_r[slot][0].start()
-        c_l[slot][1].start()
-        c_r[slot][1].start()
-        c_l[slot][0].start()
-
-    send_context(OWN)
-
-    for copy in in_push[0]:
-        copy.start()
-    out_push[0].start()
-
-    tok_r[1].wait_recv()
-    tok_l[0].wait_recv()
-    norm_rows(token_row, ROW_ATTN, nb, RT * seq, 2 * seq)
-    project(0, nb, RT, 2)
-    attend(0, RT, 2)
-    send_context(RT)
-    send_context(LT)
-
-    spread_far_wo(0)
-    tok_fr.wait_recv()
-    tok_fl.wait_recv()
-    norm_rows(token_row, ROW_ATTN, nb, OP * seq, seq)
-    project(0, nb, OP, 1)
-    attend(0, OP, 1)
-    send_context(OP)
-
-    def add_context(layer, src, slot, count, first):
-        for j in range(0, d_model, chip_cols):
-            col = pl.ds(j, chip_cols)
-            y = dot(cb[src, rows(slot, count), :], wob[layer, src, :, col])
-            if first:
-                hb[rows(slot, count), col] = tokb[rows(slot, count), col].astype(F32) + y
-            else:
-                hb[rows(slot, count), col] += y
+
+    def send_context(to_right, to_left):
+        c_r[to_right][0].start()
+        c_l[to_left][1].start()
+        c_r[to_right][1].start()
+        c_l[to_left][0].start()
 
     c_fr, c_fl = {}, {}
 
@@ -343,23 +315,43 @@
         c_l[slot][1].wait_recv()
         c_fl[slot].start()
 
+    send_context(OWN, OWN)
+
+    for copy in in_push[0]:
+        copy.start()
+    out_push[0].start()
+
+    spread_far_wo(0)
+    tok_r[1].wait_recv()
+    tok_l[0].wait_recv()
+    norm_rows(token_row, ROW_ATTN, nb, RT * seq, 2 * seq)
+    project(0, nb, RT, 2)
+    attend(0, RT, 2)
+    send_context(LT, RT)
+    send_context(RT, LT)
+
     forward_context(OWN)
+    tok_fr.wait_recv()
+    tok_fl.wait_recv()
+    norm_rows(token_row, ROW_ATTN, nb, OP * seq, seq)
+    project(0, nb, OP, 1)
+    attend(0, OP, 1)
+    send_context(OP, OP)
+
+    def add_context(slot, count):
+        for j in range(0, d_model, chip_cols):
+            col = pl.ds(j, chip_cols)
+            y = tokb[rows(slot, count), col].astype(F32)
+            for src in (OWN, RT, LT, OP):
+                y += dot(cb[src, rows(slot, count), :], wob[0, src, :, col])
+            hb[rows(slot, count), col] = y
+
+    share_wo_near(0)
+    forward_context(LT)
+    forward_context(RT)
+    share_wo_far(0)
     wo_loads[0].wait()
     wo_push[0].wait_recv()
-    add_context(0, OWN, OWN, 4, True)
-    forward_context(RT)
-    forward_context(LT)
-    share_wo_near(0)
-    forward_context(OP)
-    share_wo_far(0)
-    for slot in (OWN, RT, LT, OP):
-        c_r[slot][1].wait_recv()
-        c_l[slot][0].wait_recv()
-    for slot in (RT, LT, OP):
-        wo_share[0][slot].wait_recv()
-    start_wo(1)
-    add_context(0, LT, OWN, 4, False)
-    add_context(0, RT, OWN, 4, False)
     for copy in in_loads[0]:
         copy.wait()
     out_loads[0].wait()
@@ -408,21 +400,37 @@
         hb[row, :] = hb[row, :] + ((pb[layer, row, :] + recv_l[layer, row, :]) + recv_r[layer, row, :])
 
     rs = scatter_copies(0)
-    for slot in (OWN, RT, LT, OP):
+    c_r[LT][1].wait_recv()
+    c_l[RT][0].wait_recv()
+    c_fr[OWN].wait_recv()
+    c_fl[OWN].wait_recv()
+    for slot in (RT, LT, OP):
+        wo_share[0][slot].wait_recv()
+    add_context(OP, 1)
+    norm_rows(hidden_row, ROW_FFN, mb.at[0], OP * seq, seq)
+    feed_forward(0, OP, 1)
+    for r in range(2):
+        rs["op_r", r].start()
+        rs["op_l", r].start()
+    forward_context(OP)
+    for slot in (OWN, OP):
+        c_r[slot][1].wait_recv()
+        c_l[slot][0].wait_recv()
+    for slot in (RT, LT):
         c_fr[slot].wait_recv()
         c_fl[slot].wait_recv()
-    add_context(0, OP, OP, 1, False)
-    norm_rows(hidden_row, ROW_FFN, mb.at[0], OP * seq, seq)
-    feed_forward(0, OP, 1)
-    for r in range(2):
-        rs["op_r", r].start()
-        rs["op_l", r].start()
-    add_context(0, OP, OWN, 3, False)
-    norm_rows(hidden_row, ROW_FFN, mb.at[0], OWN * seq, 3 * seq)
+    add_context(RT, 2)
+    norm_rows(hidden_row, ROW_FFN, mb.at[0], RT * seq, 2 * seq)
     feed_forward(0, RT, 2)
     rs["plain_r", 0].start()
     rs["plain_l", 0].start()
     forward_wo(1)
+    c_r[RT][1].wait_recv()
+    c_l[LT][0].wait_recv()
+    c_fr[OP].wait_recv()
+    c_fl[OP].wait_recv()
+    add_context(OWN, 1)
+    norm_rows(hidden_row, ROW_FFN, mb.at[0], OWN * seq, seq)
     feed_forward(0, OWN, 1)
     pass_on(0, rs, 0)
     rs["plain_r", 1].start()
@@ -482,7 +490,9 @@
     attend(1, RT, 2)
     ctx_r = remote(cb.at[0, rows(RT), :], c1b.at[LT], right)
     ctx_l = remote(cb.at[0, rows(LT), :], c1b.at[RT], left)
-    ctx_o = remote(cb.at[0, rows(OP), :], c1b.at[OP], opposite)
+    half_rows = lambda r: pl.ds(r * rows_half, rows_half)
+    ctx_o = [remote(cb.at[0, pl.ds(OP * seq + r * rows_half, rows_half), :], c1b.at[OP, half_rows(r), :], opposite)
+             for r in range(2)]
     ctx_r.start()
     ctx_l.start()
     for r in range(2):
@@ -490,26 +500,33 @@
         n_gather[r][3].wait_recv()
     project(1, mb.at[2], OP, 1)
     attend(1, OP, 1)
-    ctx_o.start()
+    for copy in ctx_o:
+        copy.start()
     wo_loads[1].wait()
     wo_push[1].wait_recv()
 
-    def add_second(src, context):
+    def add_second(src, context, r=None):
+        row = rows(OWN) if r is None else half_rows(r)
         for j in range(0, d_model, chip_cols):
             col = pl.ds(j, chip_cols)
-            hb[rows(OWN), col] += dot(context, wob[1, src, :, col])
+            hb[row, col] += dot(context, wob[1, src, :, col])
 
     add_second(OWN, cb[0, rows(OWN), :])
-    for slot, copy in ((LT, ctx_r), (RT, ctx_l), (OP, ctx_o)):
+    for slot, copy in ((LT, ctx_r), (RT, ctx_l)):
         wo_share[1][slot].wait_recv()
         copy.wait_recv()
         add_second(slot, c1b[slot])
-    norm_rows(hidden_row, ROW_FFN + 1, mb.at[1], OWN * seq, seq)
+    wo_share[1][OP].wait_recv()
     m_gather = [gather_copies(mb.at[1], r) for r in range(2)]
-    for first, second in ((0, 1), (1, 0)):
-        for r in range(2):
-            m_gather[r][0][first].start()
-            m_gather[r][1][second].start()
+    for r in range(2):
+        ctx_o[r].wait_recv()
+        add_second(OP, c1b[OP, half_rows(r), :], r)
+        norm_rows(hidden_row, ROW_FFN + 1, mb.at[1], r * rows_half, rows_half)
+        to_right, to_left, _, _ = m_gather[r]
+        to_right[0].start()
+        to_left[1].start()
+        to_right[1].start()
+        to_left[0].start()
     for copy in in_loads[1]:
         copy.wait()
     out_loads[1].wait()

time: 97.7 us -> 98.7 us (1.010)
  Pallas kernels: 96.1 us -> 97.1 us
    pallas_call x1, Pallas kernels: 96.1 us -> 97.1 us  [encode(): pl.pallas_call(functools.partial(kernel, n, groups), out_shape=pltpu.VMEM...]
where the time goes in v4:
time: 98.7 us; the launch traced here: 98.6 us
  Pallas kernels  97.1 us (98%)
    pallas_call x1, Pallas kernels, encode(): pl.pallas_call(functools.partial(kernel, n, groups), out_shape=pltpu.VMEM...  97.1 us

profile of v4, /device:TPU:80, one launch (start us, length us, event | category | flops | bytes accessed | tf_op | source)
XLA Modules:
  0.0 98.6 jit_solution(4359345392714119932)
XLA Ops:
  0.7 97.1 %shard_map.127 = bf16[128,1024]{1,0:T(8,128)(2,1)S(1)} custom-call(s32[1]{0:T(128)} %copy.14.lengths, bf16[2,128]{1,0:T(2,128)(2,1)} %attn_gain.1, bf16[2,128]{1,0:T(2,128)(2,1)} %ffn_gain.1, bf16[1,128]{1,0:T(2,128)(2,1)} %bitcast.13, bf16[4,32]{1,0:T(4,128)(2,1)} %bitcast.12, bf16[1,128,1024]{2,1,0:T(8,128)(2,1)} %tok.1, bf16[2,1024,128]{2,1,0:T(8,128)(2,1)} %wq.1, ...), custom_call_target="tpu_custom_call" | custom-call | tf_op jit(solution)/shard_map/pallas_call | solution.py:601
  97.8 0.8 select_bitcast_fusion
  (1 shorter events, 0.0 us)

commit v5 on v4

--- a/solution.py
+++ b/solution.py
@@ -180,15 +180,14 @@
     out_push = [remote(wout.at[layer], woutb.at[layer, pl.ds(ff_share, ff_share), :], partner) for layer in range(layers)]
     wo_push = [remote(wo.at[layer], wob.at[layer, OWN, pl.ds(share, share), :], partner) for layer in range(layers)]
 
+    for copy in small_sends:
+        copy.start()
     start_wo(0)
     tok_load.wait()
     tok_r[0].start()
     tok_l[1].start()
-    for copy in small_sends:
-        copy.start()
     tok_r[1].start()
     tok_l[0].start()
-    start_wo(1)
     for copy in qkv_push[0]:
         copy.start()
     wo_push[0].start()
@@ -337,6 +336,7 @@
     project(0, nb, OP, 1)
     attend(0, OP, 1)
     send_context(OP, OP)
+    start_wo(1)
 
     def add_context(slot, count):
         for j in range(0, d_model, chip_cols):
@@ -346,9 +346,9 @@
                 y += dot(cb[src, rows(slot, count), :], wob[0, src, :, col])
             hb[rows(slot, count), col] = y
 
-    share_wo_near(0)
     forward_context(LT)
     forward_context(RT)
+    share_wo_near(0)
     share_wo_far(0)
     wo_loads[0].wait()
     wo_push[0].wait_recv()
@@ -409,10 +409,10 @@
     add_context(OP, 1)
     norm_rows(hidden_row, ROW_FFN, mb.at[0], OP * seq, seq)
     feed_forward(0, OP, 1)
+    forward_context(OP)
     for r in range(2):
         rs["op_r", r].start()
         rs["op_l", r].start()
-    forward_context(OP)
     for slot in (OWN, OP):
         c_r[slot][1].wait_recv()
         c_l[slot][0].wait_recv()

time: 98.7 us -> 99.4 us (level)
  the two profiles are of different devices: /device:TPU:80 before, /device:TPU:81 now
where the time goes in v5:
time: 99.4 us
  Pallas kernels  97.9 us (98%)
    pallas_call x1, Pallas kernels, encode(): pl.pallas_call(functools.partial(kernel, n, groups), out_shape=pltpu.VMEM...  97.9 us

profile of v5, /device:TPU:81, one launch (start us, length us, event | category | flops | bytes accessed | tf_op | source)
XLA Modules:
  0.0 99.4 jit_solution(7639312323279926416)
XLA Ops:
  0.7 97.9 %shard_map.127 = bf16[128,1024]{1,0:T(8,128)(2,1)S(1)} custom-call(s32[1]{0:T(128)} %copy.14.lengths, bf16[2,128]{1,0:T(2,128)(2,1)} %attn_gain.1, bf16[2,128]{1,0:T(2,128)(2,1)} %ffn_gain.1, bf16[1,128]{1,0:T(2,128)(2,1)} %bitcast.13, bf16[4,32]{1,0:T(4,128)(2,1)} %bitcast.12, bf16[1,128,1024]{2,1,0:T(8,128)(2,1)} %tok.1, bf16[2,1024,128]{2,1,0:T(8,128)(2,1)} %wq.1, ...), custom_call_target="tpu_custom_call" | custom-call | tf_op jit(solution)/shard_map/pallas_call | solution.py:601
  98.6 0.8 select_bitcast_fusion
  (1 shorter events, 0.0 us)

commit v6 on v5

--- a/solution.py
+++ b/solution.py
@@ -173,12 +173,15 @@
     tok_src = lambda c: part(tokb, OWN, None, c)
     tok_dst = lambda slot, c: part(tokb, slot, None, c)
     tok_r, tok_l = block_sends(tok_src, tok_dst)
-    qkv_push = [[remote(w.at[layer], wqkvb.at[layer, :, pl.ds(i * chip_cols + share, share)], partner)
-                 for i, w in enumerate((wq, wk, wv))] for layer in range(layers)]
-    in_push = [[remote(w.at[layer], winb.at[layer, i, pl.ds(ff_share, ff_share), :], partner) for i, w in enumerate((win0, win1))]
+    def to_partner(ref):
+        return lambda own, other: remote(ref(own), ref(other), partner)
+
+    qkv_push = [[to_partner(lambda o, i=i: wqkvb.at[layer, :, pl.ds(i * chip_cols + o * share, share)])(0, 1)
+                 for i in range(3)] for layer in range(layers)]
+    in_push = [[to_partner(lambda o, i=i: winb.at[layer, i, pl.ds(o * ff_share, ff_share), :])(0, 1) for i in range(2)]
                for layer in range(layers)]
-    out_push = [remote(wout.at[layer], woutb.at[layer, pl.ds(ff_share, ff_share), :], partner) for layer in range(layers)]
-    wo_push = [remote(wo.at[layer], wob.at[layer, OWN, pl.ds(share, share), :], partner) for layer in range(layers)]
+    out_push = [to_partner(lambda o: woutb.at[layer, pl.ds(o * ff_share, ff_share), :])(0, 1) for layer in range(layers)]
+    wo_push = [to_partner(lambda o: wob.at[layer, OWN, pl.ds(o * share, share), :])(0, 1) for layer in range(layers)]
 
     for copy in small_sends:
         copy.start()
@@ -188,9 +191,16 @@
     tok_l[1].start()
     tok_r[1].start()
     tok_l[0].start()
-    for copy in qkv_push[0]:
+    for load_copy, copy in zip(qkv_loads[0], qkv_push[0]):
+        load_copy.wait()
         copy.start()
+    wo_loads[0].wait()
     wo_push[0].start()
+    for load_copy, copy in zip(in_loads[0], in_push[0]):
+        load_copy.wait()
+        copy.start()
+    out_loads[0].wait()
+    out_push[0].start()
 
     sm_all[me] = smalls[...]
     for copy in small_sends:
@@ -273,8 +283,6 @@
 
     norm_rows(token_row, ROW_ATTN, nb, OWN * seq, seq)
     build_bias()
-    for copy in qkv_loads[0]:
-        copy.wait()
     for copy in qkv_push[0]:
         copy.wait_recv()
     project(0, nb, OWN, 1)
@@ -316,10 +324,6 @@
 
     send_context(OWN, OWN)
 
-    for copy in in_push[0]:
-        copy.start()
-    out_push[0].start()
-
     spread_far_wo(0)
     tok_r[1].wait_recv()
     tok_l[0].wait_recv()
@@ -350,11 +354,7 @@
     forward_context(RT)
     share_wo_near(0)
     share_wo_far(0)
-    wo_loads[0].wait()
     wo_push[0].wait_recv()
-    for copy in in_loads[0]:
-        copy.wait()
-    out_loads[0].wait()
     for copy in in_push[0]:
         copy.wait_recv()
     out_push[0].wait_recv()
@@ -437,11 +437,15 @@
     rs["plain_l", 1].start()
     pass_on(0, rs, 1)
     spread_far_wo(1)
-    for copy in qkv_push[1]:
+    for load_copy, copy in zip(qkv_loads[1], qkv_push[1]):
+        load_copy.wait()
         copy.start()
+    wo_loads[1].wait()
     wo_push[1].start()
-    for copy in in_push[1]:
+    for load_copy, copy in zip(in_loads[1], in_push[1]):
+        load_copy.wait()
         copy.start()
+    out_loads[1].wait()
     out_push[1].start()
 
     def gather_copies(ref, r):
@@ -469,8 +473,6 @@
         fl.start()
 
     forward_gather(n_gather[0])
-    for copy in qkv_loads[1]:
-        copy.wait()
     for copy in qkv_push[1]:
         copy.wait_recv()
     for copies in c_r, c_l:
@@ -502,7 +504,6 @@
     attend(1, OP, 1)
     for copy in ctx_o:
         copy.start()
-    wo_loads[1].wait()
     wo_push[1].wait_recv()
 
     def add_second(src, context, r=None):
@@ -527,9 +528,6 @@
         to_left[1].start()
         to_right[1].start()
         to_left[0].start()
-    for copy in in_loads[1]:
-        copy.wait()
-    out_loads[1].wait()
     for copy in in_push[1]:
         copy.wait_recv()
     out_push[1].wait_recv()

time: 99.4 us -> 99.4 us (level)
  no operation moved by 1% of the time
where the time goes in v6:
time: 99.4 us; the launch traced here: 99.3 us
  Pallas kernels  97.8 us (98%)
    pallas_call x1, Pallas kernels, encode(): pl.pallas_call(functools.partial(kernel, n, groups), out_shape=pltpu.VMEM...  97.8 us

profile of v6, /device:TPU:81, one launch (start us, length us, event | category | flops | bytes accessed | tf_op | source)
XLA Modules:
  0.0 99.3 jit_solution(2220424023241256285)
XLA Ops:
  0.7 97.8 %shard_map.127 = bf16[128,1024]{1,0:T(8,128)(2,1)S(1)} custom-call(s32[1]{0:T(128)} %copy.14.lengths, bf16[2,128]{1,0:T(2,128)(2,1)} %attn_gain.1, bf16[2,128]{1,0:T(2,128)(2,1)} %ffn_gain.1, bf16[1,128]{1,0:T(2,128)(2,1)} %bitcast.13, bf16[4,32]{1,0:T(4,128)(2,1)} %bitcast.12, bf16[1,128,1024]{2,1,0:T(8,128)(2,1)} %tok.1, bf16[2,1024,128]{2,1,0:T(8,128)(2,1)} %wq.1, ...), custom_call_target="tpu_custom_call" | custom-call | tf_op jit(solution)/shard_map/pallas_call | solution.py:599
  98.5 0.8 select_bitcast_fusion
  (1 shorter events, 0.0 us)

commit v7 on v6

--- a/solution.py
+++ b/solution.py
@@ -42,7 +42,7 @@
 
 
 def kernel(n, groups, lengths, attn_gain, ffn_gain, final_gain, bias_table, tok, wq, wk, wv, wo, win0, win1, wout, out,
-           smalls, sm_all, gainb, lenb, biasb, tokb, nb, mb, wqkvb, wob, winb, woutb, qb, kb, vb, cb, c1b, hb, pb,
+           smalls, sm_all, gainb, lenb, biasb, tokb, nb, mb, wqkvb, wob, winb, woutb, qb, kb, vb, cb, c1b, relay_c, hb, pb,
            relay_a, relay_b, recv_l, recv_r, send_sem, recv_sem, load_sem):
     seq, d_model = tok.shape[1], tok.shape[2]
     layers = wq.shape[0]
@@ -82,12 +82,12 @@
         return ref.at[row, col]
 
     tok_load = load(tok.at[0], tokb.at[rows(OWN), :])
+    wo_loads = [load(wo.at[layer], wob.at[layer, OWN, pl.ds(0, share), :]) for layer in range(layers)]
     qkv_loads = []
     for layer in range(layers):
         qkv_loads.append([load(w.at[layer], wqkvb.at[layer, :, pl.ds(i * chip_cols, share)])
                           for i, w in enumerate((wq, wk, wv))])
         if layer == 0:
-            wo_loads = [load(wo.at[k], wob.at[k, OWN, pl.ds(0, share), :]) for k in range(layers)]
             in_loads = []
             out_loads = []
         in_loads.append([load(w.at[layer], winb.at[layer, i, pl.ds(0, ff_share), :]) for i, w in enumerate((win0, win1))])
@@ -123,7 +123,7 @@
 
     def wo_copies(layer):
         col = lambda c: pl.ds(pl.multiple_of(piece_col + c * (piece_cols // 2), LANES), piece_cols // 2)
-        src = lambda c: wo.at[layer, pl.ds(piece_row, piece_rows), col(c)]
+        src = lambda c: wob.at[layer, OWN, pl.ds(piece_row, piece_rows), col(c)]
         dst = lambda slot, c: wob.at[layer, slot, pl.ds(piece_row, piece_rows), col(c)]
         to_right, to_left = block_sends(src, dst)
         fr, fl = block_forwards(dst)
@@ -185,16 +185,15 @@
 
     for copy in small_sends:
         copy.start()
+    for copy in wo_loads:
+        copy.wait()
     start_wo(0)
     tok_load.wait()
     tok_r[0].start()
     tok_l[1].start()
-    tok_r[1].start()
-    tok_l[0].start()
     for load_copy, copy in zip(qkv_loads[0], qkv_push[0]):
         load_copy.wait()
         copy.start()
-    wo_loads[0].wait()
     wo_push[0].start()
     for load_copy, copy in zip(in_loads[0], in_push[0]):
         load_copy.wait()
@@ -289,6 +288,8 @@
     attend(0, OWN, 1)
 
     forward_wo(0)
+    tok_r[1].start()
+    tok_l[0].start()
     tok_fr, tok_fl = block_forwards(tok_dst)
     tok_r[0].wait_recv()
     tok_fr.start()
@@ -440,7 +441,6 @@
     for load_copy, copy in zip(qkv_loads[1], qkv_push[1]):
         load_copy.wait()
         copy.start()
-    wo_loads[1].wait()
     wo_push[1].start()
     for load_copy, copy in zip(in_loads[1], in_push[1]):
         load_copy.wait()
@@ -493,8 +493,13 @@
     ctx_r = remote(cb.at[0, rows(RT), :], c1b.at[LT], right)
     ctx_l = remote(cb.at[0, rows(LT), :], c1b.at[RT], left)
     half_rows = lambda r: pl.ds(r * rows_half, rows_half)
-    ctx_o = [remote(cb.at[0, pl.ds(OP * seq + r * rows_half, rows_half), :], c1b.at[OP, half_rows(r), :], opposite)
-             for r in range(2)]
+
+    def far_context(r, p, device):
+        col = pl.ds(p * LANES, LANES)
+        out_copy = remote(cb.at[0, pl.ds(OP * seq + r * rows_half, rows_half), col], relay_c.at[p, half_rows(r), :], device)
+        return out_copy, remote(relay_c.at[p, half_rows(r), :], c1b.at[OP, half_rows(r), col], device)
+
+    ctx_o = [[far_context(r, p, device) for p, device in ((0, right), (1, left))] for r in range(2)]
     ctx_r.start()
     ctx_l.start()
     for r in range(2):
@@ -502,8 +507,13 @@
         n_gather[r][3].wait_recv()
     project(1, mb.at[2], OP, 1)
     attend(1, OP, 1)
-    for copy in ctx_o:
-        copy.start()
+    for r in range(2):
+        for copy, _ in ctx_o[r]:
+            copy.start()
+    for r in range(2):
+        for copy, onward in ctx_o[r]:
+            copy.wait_recv()
+            onward.start()
     wo_push[1].wait_recv()
 
     def add_second(src, context, r=None):
@@ -520,7 +530,8 @@
     wo_share[1][OP].wait_recv()
     m_gather = [gather_copies(mb.at[1], r) for r in range(2)]
     for r in range(2):
-        ctx_o[r].wait_recv()
+        for _, onward in ctx_o[r]:
+            onward.wait_recv()
         add_second(OP, c1b[OP, half_rows(r), :], r)
         norm_rows(hidden_row, ROW_FFN + 1, mb.at[1], r * rows_half, rows_half)
         to_right, to_left, _, _ = m_gather[r]
@@ -586,6 +597,7 @@
         pltpu.VMEM((2, ring * seq, chip_cols), BF16),
         pltpu.VMEM((ring, ring * seq, chip_cols), BF16),
         pltpu.VMEM((ring, seq, chip_cols), BF16),
+        pltpu.VMEM((2, seq, LANES), BF16),
         pltpu.VMEM((ring * seq, d_model), F32),
         pltpu.VMEM((layers, ring * seq, d_model), F32),
         pltpu.VMEM((layers, seq, d_model // 2), F32),

time: 99.4 us -> 100 us (level); the launches traced: 99.3 us -> 98.4 us
  no operation moved by 1% of the time
where the time goes in v7:
time: 100 us; the launch traced here: 98.4 us
  Pallas kernels  96.9 us (97%)
    pallas_call x1, Pallas kernels, encode(): pl.pallas_call(functools.partial(kernel, n, groups), out_shape=pltpu.VMEM...  96.9 us

profile of v7, /device:TPU:81, one launch (start us, length us, event | category | flops | bytes accessed | tf_op | source)
XLA Modules:
  0.0 98.4 jit_solution(13682450766091053715)
XLA Ops:
  0.7 96.9 %shard_map.127 = bf16[128,1024]{1,0:T(8,128)(2,1)S(1)} custom-call(s32[1]{0:T(128)} %copy.14.lengths, bf16[2,128]{1,0:T(2,128)(2,1)} %attn_gain.1, bf16[2,128]{1,0:T(2,128)(2,1)} %ffn_gain.1, bf16[1,128]{1,0:T(2,128)(2,1)} %bitcast.13, bf16[4,32]{1,0:T(4,128)(2,1)} %bitcast.12, bf16[1,128,1024]{2,1,0:T(8,128)(2,1)} %tok.1, bf16[2,1024,128]{2,1,0:T(8,128)(2,1)} %wq.1, ...), custom_call_target="tpu_custom_call" | custom-call | tf_op jit(solution)/shard_map/pallas_call | solution.py:611
  97.6 0.8 select_bitcast_fusion
  (1 shorter events, 0.0 us)

commit v8 on v6

--- a/solution.py
+++ b/solution.py
@@ -41,8 +41,9 @@
     return lax.dot_general(a, b, (((1,), (1,)), ((), ())), preferred_element_type=F32)
 
 
-def kernel(n, groups, lengths, attn_gain, ffn_gain, final_gain, bias_table, tok, wq, wk, wv, wo, win0, win1, wout, out,
-           smalls, sm_all, gainb, lenb, biasb, tokb, nb, mb, wqkvb, wob, winb, woutb, qb, kb, vb, cb, c1b, hb, pb,
+def kernel(n, groups, lengths_in, attn_gain_in, ffn_gain_in, final_gain_in, bias_table_in,
+           tok, wq, wk, wv, wo, win0, win1, wout, out,
+           lengths, attn_gain, ffn_gain, final_gain, bias_table, smalls, sm_all, gainb, lenb, biasb, tokb, nb, mb, wqkvb, wob, winb, woutb, qb, kb, vb, cb, c1b, hb, pb,
            relay_a, relay_b, recv_l, recv_r, send_sem, recv_sem, load_sem):
     seq, d_model = tok.shape[1], tok.shape[2]
     layers = wq.shape[0]
@@ -81,30 +82,36 @@
         col = slice(None) if c is None else pl.ds(c * half, half)
         return ref.at[row, col]
 
+    barrier = pltpu.get_barrier_semaphore()
+    for k in range(1, n):
+        pl.semaphore_signal(barrier, inc=1, device_id={"fsdp": lax.rem(me + k, n)}, device_id_type=MESH)
+    for k in range(1, groups):
+        pl.semaphore_signal(barrier, inc=1, device_id={"dp": lax.rem(group + k, groups)}, device_id_type=MESH)
+
+    small_loads = [load(src, dst) for src, dst in zip(
+        (lengths_in, attn_gain_in, ffn_gain_in, final_gain_in, bias_table_in),
+        (lengths, attn_gain, ffn_gain, final_gain, bias_table))]
     tok_load = load(tok.at[0], tokb.at[rows(OWN), :])
+    wo_loads = [load(wo.at[layer], wob.at[layer, OWN, pl.ds(0, share), :]) for layer in range(layers)]
     qkv_loads = []
     for layer in range(layers):
         qkv_loads.append([load(w.at[layer], wqkvb.at[layer, :, pl.ds(i * chip_cols, share)])
                           for i, w in enumerate((wq, wk, wv))])
         if layer == 0:
-            wo_loads = [load(wo.at[k], wob.at[k, OWN, pl.ds(0, share), :]) for k in range(layers)]
             in_loads = []
             out_loads = []
         in_loads.append([load(w.at[layer], winb.at[layer, i, pl.ds(0, ff_share), :]) for i, w in enumerate((win0, win1))])
         out_loads.append(load(wout.at[layer], woutb.at[layer, pl.ds(0, ff_share), :]))
 
+    for copy in small_loads:
+        copy.wait()
     smalls[ROW_ATTN:ROW_ATTN + layers, :] = attn_gain[...].astype(F32)
     smalls[ROW_FFN:ROW_FFN + layers, :] = ffn_gain[...].astype(F32)
     smalls[ROW_FINAL:ROW_FINAL + 1, :] = final_gain[...].astype(F32)
     table = bias_table[...].astype(F32)
     smalls[ROW_BIAS:ROW_BIAS + 1, :] = jnp.concatenate([table[i:i + 1] for i in range(table.shape[0])], axis=1)
-    smalls[ROW_LEN:SMALL_ROWS, :] = jnp.full((SMALL_ROWS - ROW_LEN, LANES), lengths[0], jnp.int32).astype(F32)
-
-    barrier = pltpu.get_barrier_semaphore()
-    for k in range(1, n):
-        pl.semaphore_signal(barrier, inc=1, device_id={"fsdp": lax.rem(me + k, n)}, device_id_type=MESH)
-    for k in range(1, groups):
-        pl.semaphore_signal(barrier, inc=1, device_id={"dp": lax.rem(group + k, groups)}, device_id_type=MESH)
+    smalls[ROW_LEN:SMALL_ROWS, :] = jnp.broadcast_to(lengths[...].astype(F32), (SMALL_ROWS - ROW_LEN, LANES))
+
     pl.semaphore_wait(barrier, n - 1 + groups - 1)
 
     def block_sends(src, dst):
@@ -123,7 +130,7 @@
 
     def wo_copies(layer):
         col = lambda c: pl.ds(pl.multiple_of(piece_col + c * (piece_cols // 2), LANES), piece_cols // 2)
-        src = lambda c: wo.at[layer, pl.ds(piece_row, piece_rows), col(c)]
+        src = lambda c: wob.at[layer, OWN, pl.ds(piece_row, piece_rows), col(c)]
         dst = lambda slot, c: wob.at[layer, slot, pl.ds(piece_row, piece_rows), col(c)]
         to_right, to_left = block_sends(src, dst)
         fr, fl = block_forwards(dst)
@@ -185,16 +192,15 @@
 
     for copy in small_sends:
         copy.start()
+    for copy in wo_loads:
+        copy.wait()
     start_wo(0)
     tok_load.wait()
     tok_r[0].start()
     tok_l[1].start()
-    tok_r[1].start()
-    tok_l[0].start()
     for load_copy, copy in zip(qkv_loads[0], qkv_push[0]):
         load_copy.wait()
         copy.start()
-    wo_loads[0].wait()
     wo_push[0].start()
     for load_copy, copy in zip(in_loads[0], in_push[0]):
         load_copy.wait()
@@ -210,7 +216,7 @@
     for slot, device in ((OWN, me), (RT, right), (LT, left), (OP, opposite)):
         lenb[slot] = jnp.broadcast_to(sm_all[device, ROW_LEN:ROW_LEN + 1, :], (8, LANES))
 
-    def norm_rows(load_row, gain_row, dst, start, count):
+    def norm_rows(load_row, gain_row, dst, start, count, masked=False):
         step = 32
 
         def body(i, carry):
@@ -218,6 +224,9 @@
             x = load_row(r, step)
             mean_sq = jnp.mean(x * x, axis=-1, keepdims=True)
             normed = x * lax.rsqrt(mean_sq + NORM_EPS) * gainb[gain_row:gain_row + 1, :]
+            if masked:
+                position = (r + lax.broadcasted_iota(jnp.int32, (step, d_model), 0)).astype(F32)
+                normed = jnp.where(position < lenb[OWN, 0:1, 0:1], normed, 0.0)
             dst[pl.ds(r, step), :] = normed.astype(BF16)
             return carry
 
@@ -289,6 +298,8 @@
     attend(0, OWN, 1)
 
     forward_wo(0)
+    tok_r[1].start()
+    tok_l[0].start()
     tok_fr, tok_fl = block_forwards(tok_dst)
     tok_r[0].wait_recv()
     tok_fr.start()
@@ -440,7 +451,6 @@
     for load_copy, copy in zip(qkv_loads[1], qkv_push[1]):
         load_copy.wait()
         copy.start()
-    wo_loads[1].wait()
     wo_push[1].start()
     for load_copy, copy in zip(in_loads[1], in_push[1]):
         load_copy.wait()
@@ -493,6 +503,7 @@
     ctx_r = remote(cb.at[0, rows(RT), :], c1b.at[LT], right)
     ctx_l = remote(cb.at[0, rows(LT), :], c1b.at[RT], left)
     half_rows = lambda r: pl.ds(r * rows_half, rows_half)
+
     ctx_o = [remote(cb.at[0, pl.ds(OP * seq + r * rows_half, rows_half), :], c1b.at[OP, half_rows(r), :], opposite)
              for r in range(2)]
     ctx_r.start()
@@ -554,7 +565,7 @@
         pass_on(1, rs, r)
     for r in range(2):
         collect(1, rs, r)
-        norm_rows(hidden_row, ROW_FINAL, out, r * rows_half, rows_half)
+        norm_rows(hidden_row, ROW_FINAL, out, r * rows_half, rows_half, masked=True)
     for copy in sent:
         if id(copy) not in done:
             copy.wait_send()
@@ -566,9 +577,13 @@
     ff_share = w_out.shape[1]
     chip_cols = 2 * share
     ring = n // 2
-    any_spec = pl.BlockSpec(memory_space=pl.ANY)
     vmem = pl.BlockSpec(memory_space=pltpu.VMEM)
     scratch = [
+        pltpu.VMEM(lengths.shape, jnp.int32),
+        pltpu.VMEM(attn_gain.shape, BF16),
+        pltpu.VMEM(ffn_gain.shape, BF16),
+        pltpu.VMEM(final_gain.shape, BF16),
+        pltpu.VMEM(bias_table.shape, BF16),
         pltpu.VMEM((SMALL_ROWS, LANES), F32),
         pltpu.VMEM((n, SMALL_ROWS, LANES), F32),
         pltpu.VMEM((8, d_model), F32),
@@ -594,12 +609,12 @@
         pltpu.VMEM((layers, seq, d_model), F32),
         pltpu.SemaphoreType.DMA((160 + 4 * groups,)),
         pltpu.SemaphoreType.DMA((160 + 4 * groups,)),
-        pltpu.SemaphoreType.DMA((24,)),
+        pltpu.SemaphoreType.DMA((32,)),
     ]
     return pl.pallas_call(
         functools.partial(kernel, n, groups),
         out_shape=pltpu.VMEM((seq, d_model), BF16),
-        in_specs=[pl.BlockSpec(memory_space=pltpu.SMEM)] + [vmem] * 4 + [any_spec] * 8,
+        in_specs=[pl.BlockSpec(memory_space=pltpu.HBM)] * 13,
         out_specs=vmem,
         scratch_shapes=scratch,
         compiler_params=pltpu.CompilerParams(
@@ -617,12 +632,10 @@
                 col_spec, col_spec, row_spec, P("fsdp"))
 
     def local_forward(tokens, lengths, attn_gain, w_q, w_k, w_v, w_o, rel_bias, ffn_gain, w_in0, w_in1, w_out, final_gain):
-        seq_len = tokens.shape[1]
         layers, buckets, heads = rel_bias.shape
         bias_table = jnp.swapaxes(rel_bias, 1, 2).reshape(layers * heads, buckets)
-        normed_out = encode(n, groups, lengths, attn_gain, ffn_gain, final_gain[None], bias_table, tokens, w_q, w_k, w_v, w_o,
+        encoded = encode(n, groups, lengths[None], attn_gain, ffn_gain, final_gain[None], bias_table, tokens, w_q, w_k, w_v, w_o,
                             jnp.swapaxes(w_in0, 1, 2), jnp.swapaxes(w_in1, 1, 2), w_out)
-        key_ok = jnp.arange(seq_len, dtype=jnp.int32)[:, None] < lengths
-        return jnp.where(key_ok, normed_out, jnp.zeros_like(normed_out))[None]
+        return encoded[None]
 
     return jax.shard_map(local_forward, mesh=mesh, in_specs=in_specs, out_specs=batch_spec, check_vma=False)

time: 99.4 us -> 97.4 us (0.980); the launches traced: 99.3 us -> 96 us
  Pallas kernels: 97.8 us -> 94.7 us
    pallas_call x1, Pallas kernels: 97.8 us -> 94.7 us  [encode(): pl.pallas_call(functools.partial(kernel, n, groups), out_shape=pltpu.VMEM...]
where the time goes in v8:
time: 97.4 us; the launch traced here: 96 us
  Pallas kernels  94.7 us (97%)
    pallas_call x1, Pallas kernels, encode(): pl.pallas_call(functools.partial(kernel, n, groups), out_shape=pltpu.VMEM...  94.7 us

profile of v8, /device:TPU:81, one launch (start us, length us, event | category | flops | bytes accessed | tf_op | source)
XLA Modules:
  0.0 96.0 jit_solution(5711805149835149966)
XLA Ops:
  0.7 94.7 %shard_map.127 = bf16[128,1024]{1,0:T(8,128)(2,1)S(1)} custom-call(s32[1,1]{1,0:T(1,128)} %bitcast.8.lengths_in, bf16[2,128]{1,0:T(2,128)(2,1)} %attn_gain_in.1, bf16[2,128]{1,0:T(2,128)(2,1)} %ffn_gain_in.1, bf16[1,128]{1,0:T(2,128)(2,1)} %bitcast.13, bf16[4,32]{1,0:T(4,128)(2,1)} %bitcast.12, bf16[1,128,1024]{2,1,0:T(8,128)(2,1)} %tok.1, ...), custom_call_target="tpu_custom_call" | custom-call | tf_op jit(solution)/shard_map/pallas_call | solution.py:614
  95.3 0.7 copy.15

commit v9 on v8

--- a/solution.py
+++ b/solution.py
@@ -130,11 +130,11 @@
 
     def wo_copies(layer):
         col = lambda c: pl.ds(pl.multiple_of(piece_col + c * (piece_cols // 2), LANES), piece_cols // 2)
-        src = lambda c: wob.at[layer, OWN, pl.ds(piece_row, piece_rows), col(c)]
         dst = lambda slot, c: wob.at[layer, slot, pl.ds(piece_row, piece_rows), col(c)]
-        to_right, to_left = block_sends(src, dst)
         fr, fl = block_forwards(dst)
         piece = lambda slot, count: wob.at[layer, pl.ds(slot, count), pl.ds(piece_row, piece_rows), pl.ds(piece_col, piece_cols)]
+        to_right = remote(piece(OWN, 1), piece(LT, 1), right)
+        to_left = remote(piece(OWN, 1), piece(RT, 1), left)
         spread = [[remote(piece(slot, count), piece(slot, count), lax.rem(group + k, groups), "dp") for k in range(1, groups)]
                   for slot, count in ((RT, 2), (OP, 1))]
         push = {s: remote(wob.at[layer, s, pl.ds(0, share), :], wob.at[layer, s, pl.ds(share, share), :], partner)
@@ -144,18 +144,14 @@
     wo_r, wo_l, wo_fr, wo_fl, wo_spread, wo_share = zip(*[wo_copies(layer) for layer in range(layers)])
 
     def start_wo(layer):
-        wo_r[layer][0].start()
-        wo_l[layer][1].start()
-        wo_r[layer][1].start()
-        wo_l[layer][0].start()
+        wo_r[layer].start()
+        wo_l[layer].start()
 
     def forward_wo(layer):
-        wo_r[layer][0].wait_recv()
+        wo_r[layer].wait_recv()
         wo_fr[layer].start()
-        wo_l[layer][1].wait_recv()
+        wo_l[layer].wait_recv()
         wo_fl[layer].start()
-        wo_r[layer][1].wait_recv()
-        wo_l[layer][0].wait_recv()
         for copy in wo_spread[layer][0]:
             copy.start()
 
@@ -312,25 +308,23 @@
     c_r, c_l = {}, {}
 
     for slot in (OWN, RT, LT, OP):
-        c_r[slot] = [remote(c_part(0, slot, p), c_part(LT, TO_RIGHT[slot], p), right) for p in range(2)]
-        c_l[slot] = [remote(c_part(0, slot, p), c_part(RT, TO_LEFT[slot], p), left) for p in range(2)]
+        c_r[slot] = remote(cb.at[0, rows(slot), :], cb.at[LT, rows(TO_RIGHT[slot]), :], right)
+        c_l[slot] = remote(cb.at[0, rows(slot), :], cb.at[RT, rows(TO_LEFT[slot]), :], left)
 
     def send_context(to_right, to_left):
-        c_r[to_right][0].start()
-        c_l[to_left][1].start()
-        c_r[to_right][1].start()
-        c_l[to_left][0].start()
+        c_r[to_right].start()
+        c_l[to_left].start()
 
     c_fr, c_fl = {}, {}
 
     def forward_context(slot):
         near, far = TO_RIGHT[slot], TO_RIGHT[TO_RIGHT[slot]]
         c_fr[slot] = remote(c_part(LT, near, 0), c_part(OP, far, 0), right)
-        c_r[slot][0].wait_recv()
+        c_r[slot].wait_recv()
         c_fr[slot].start()
         near, far = TO_LEFT[slot], TO_LEFT[TO_LEFT[slot]]
         c_fl[slot] = remote(c_part(RT, near, 1), c_part(OP, far, 1), left)
-        c_l[slot][1].wait_recv()
+        c_l[slot].wait_recv()
         c_fl[slot].start()
 
     send_context(OWN, OWN)
@@ -411,8 +405,6 @@
         hb[row, :] = hb[row, :] + ((pb[layer, row, :] + recv_l[layer, row, :]) + recv_r[layer, row, :])
 
     rs = scatter_copies(0)
-    c_r[LT][1].wait_recv()
-    c_l[RT][0].wait_recv()
     c_fr[OWN].wait_recv()
     c_fl[OWN].wait_recv()
     for slot in (RT, LT, OP):
@@ -424,9 +416,6 @@
     for r in range(2):
         rs["op_r", r].start()
         rs["op_l", r].start()
-    for slot in (OWN, OP):
-        c_r[slot][1].wait_recv()
-        c_l[slot][0].wait_recv()
     for slot in (RT, LT):
         c_fr[slot].wait_recv()
         c_fl[slot].wait_recv()
@@ -436,8 +425,6 @@
     rs["plain_r", 0].start()
     rs["plain_l", 0].start()
     forward_wo(1)
-    c_r[RT][1].wait_recv()
-    c_l[LT][0].wait_recv()
     c_fr[OP].wait_recv()
     c_fl[OP].wait_recv()
     add_context(OWN, 1)
@@ -487,9 +474,8 @@
         copy.wait_recv()
     for copies in c_r, c_l:
         for slot in (OWN, RT, LT, OP):
-            for copy in copies[slot]:
-                copy.wait_send()
-                done.add(id(copy))
+            copies[slot].wait_send()
+            done.add(id(copies[slot]))
     project(1, mb.at[2], OWN, 1)
     attend(1, OWN, 1)
     forward_gather(n_gather[1])

time: 97.4 us -> 99.2 us (1.018); the launches traced: 96 us -> 99.1 us
  Pallas kernels: 94.7 us -> 97.7 us
    pallas_call x1, Pallas kernels: 94.7 us -> 97.7 us  [encode(): pl.pallas_call(functools.partial(kernel, n, groups), out_shape=pltpu.VMEM...]
where the time goes in v9:
time: 99.2 us; the launch traced here: 99.1 us
  Pallas kernels  97.7 us (98%)
    pallas_call x1, Pallas kernels, encode(): pl.pallas_call(functools.partial(kernel, n, groups), out_shape=pltpu.VMEM...  97.7 us

profile of v9, /device:TPU:81, one launch (start us, length us, event | category | flops | bytes accessed | tf_op | source)
XLA Modules:
  0.0 99.1 jit_solution(11199830937264492399)
XLA Ops:
  0.7 97.7 %shard_map.127 = bf16[128,1024]{1,0:T(8,128)(2,1)S(1)} custom-call(s32[1,1]{1,0:T(1,128)} %bitcast.8.lengths_in, bf16[2,128]{1,0:T(2,128)(2,1)} %attn_gain_in.1, bf16[2,128]{1,0:T(2,128)(2,1)} %ffn_gain_in.1, bf16[1,128]{1,0:T(2,128)(2,1)} %bitcast.13, bf16[4,32]{1,0:T(4,128)(2,1)} %bitcast.12, bf16[1,128,1024]{2,1,0:T(8,128)(2,1)} %tok.1, ...), custom_call_target="tpu_custom_call" | custom-call | tf_op jit(solution)/shard_map/pallas_call | solution.py:600
  98.4 0.7 copy.15

commit v10 on v8

--- a/solution.py
+++ b/solution.py
@@ -11,6 +11,7 @@
 NUM_BUCKETS = 32
 NORM_EPS = 1e-6
 LANES = 128
+ROW_PARTS = 4
 MASKED = -1e30
 MESH = pl.DeviceIdType.MESH
 BF16 = jnp.bfloat16
@@ -47,7 +48,7 @@
            relay_a, relay_b, recv_l, recv_r, send_sem, recv_sem, load_sem):
     seq, d_model = tok.shape[1], tok.shape[2]
     layers = wq.shape[0]
-    half, rows_half = d_model // 2, seq // 2
+    half, rows_part = d_model // 2, seq // ROW_PARTS
     share, ff_share = wq.shape[2], wout.shape[1]
     chip_cols = 2 * share
 
@@ -78,7 +79,7 @@
         return pl.ds(slot * seq, count * seq)
 
     def part(ref, slot, r, c):
-        row = pl.ds(slot * seq, seq) if r is None else pl.ds(slot * seq + r * rows_half, rows_half)
+        row = pl.ds(slot * seq, seq) if r is None else pl.ds(slot * seq + r * rows_part, rows_part)
         col = slice(None) if c is None else pl.ds(c * half, half)
         return ref.at[row, col]
 
@@ -177,9 +178,22 @@
         wo_share[layer][OP].start()
 
     small_sends = [remote(smalls, sm_all.at[me], lax.rem(me + k, n)) for k in range(1, n)]
-    tok_src = lambda c: part(tokb, OWN, None, c)
-    tok_dst = lambda slot, c: part(tokb, slot, None, c)
-    tok_r, tok_l = block_sends(tok_src, tok_dst)
+    def gather_copies(ref, r):
+        to_right = [remote(part(ref, OWN, r, c), part(ref, LT, r, c), right) for c in range(2)]
+        to_left = [remote(part(ref, OWN, r, c), part(ref, RT, r, c), left) for c in range(2)]
+        fr = remote(part(ref, LT, r, 0), part(ref, OP, r, 0), right)
+        fl = remote(part(ref, RT, r, 1), part(ref, OP, r, 1), left)
+        return to_right, to_left, fr, fl
+
+    def forward_gather(gather):
+        to_right, to_left, fr, fl = gather
+        to_right[0].wait_recv()
+        fr.start()
+        to_left[1].wait_recv()
+        fl.start()
+
+    tok_gather = [gather_copies(tokb, r) for r in range(ROW_PARTS)]
+
     def to_partner(ref):
         return lambda own, other: remote(ref(own), ref(other), partner)
 
@@ -196,8 +210,9 @@
         copy.wait()
     start_wo(0)
     tok_load.wait()
-    tok_r[0].start()
-    tok_l[1].start()
+    for to_right, to_left, _, _ in tok_gather:
+        to_right[0].start()
+        to_left[1].start()
     for load_copy, copy in zip(qkv_loads[0], qkv_push[0]):
         load_copy.wait()
         copy.start()
@@ -298,13 +313,11 @@
     attend(0, OWN, 1)
 
     forward_wo(0)
-    tok_r[1].start()
-    tok_l[0].start()
-    tok_fr, tok_fl = block_forwards(tok_dst)
-    tok_r[0].wait_recv()
-    tok_fr.start()
-    tok_l[1].wait_recv()
-    tok_fl.start()
+    for to_right, to_left, _, _ in tok_gather:
+        to_right[1].start()
+        to_left[0].start()
+    for gather in tok_gather:
+        forward_gather(gather)
 
     def c_part(src, slot, pair):
         return cb.at[src, rows(slot), pl.ds(pair * LANES, LANES)]
@@ -336,8 +349,9 @@
     send_context(OWN, OWN)
 
     spread_far_wo(0)
-    tok_r[1].wait_recv()
-    tok_l[0].wait_recv()
+    for to_right, to_left, _, _ in tok_gather:
+        to_right[1].wait_recv()
+        to_left[0].wait_recv()
     norm_rows(token_row, ROW_ATTN, nb, RT * seq, 2 * seq)
     project(0, nb, RT, 2)
     attend(0, RT, 2)
@@ -345,8 +359,9 @@
     send_context(RT, LT)
 
     forward_context(OWN)
-    tok_fr.wait_recv()
-    tok_fl.wait_recv()
+    for _, _, fr, fl in tok_gather:
+        fr.wait_recv()
+        fl.wait_recv()
     norm_rows(token_row, ROW_ATTN, nb, OP * seq, seq)
     project(0, nb, OP, 1)
     attend(0, OP, 1)
@@ -382,9 +397,9 @@
     def scatter_copies(layer):
         p, ra, rb = pb.at[layer], relay_a.at[layer], relay_b.at[layer]
         rl, rr = recv_l.at[layer], recv_r.at[layer]
-        row = lambda r: pl.ds(r * rows_half, rows_half)
+        row = lambda r: pl.ds(r * rows_part, rows_part)
         copies = {}
-        for r in range(2):
+        for r in range(ROW_PARTS):
             copies["op_r", r] = remote(part(p, OP, r, 0), ra.at[row(r), :], right)
             copies["op_l", r] = remote(part(p, OP, r, 1), rb.at[row(r), :], left)
             copies["plain_r", r] = remote(part(p, RT, r, 1), part(rl, 0, r, 1), right)
@@ -394,9 +409,9 @@
         return copies
 
     def pass_on(layer, copies, r):
-        a = pl.ds(RT * seq + r * rows_half, rows_half)
-        b = pl.ds(LT * seq + r * rows_half, rows_half)
-        row = pl.ds(r * rows_half, rows_half)
+        a = pl.ds(RT * seq + r * rows_part, rows_part)
+        b = pl.ds(LT * seq + r * rows_part, rows_part)
+        row = pl.ds(r * rows_part, rows_part)
         copies["op_r", r].wait_recv()
         pb[layer, a, 0:half] += relay_a[layer, row, :]
         copies["sum_r", r].start()
@@ -407,7 +422,7 @@
     def collect(layer, copies, r):
         for name in ("plain_r", "plain_l", "sum_r", "sum_l"):
             copies[name, r].wait_recv()
-        row = pl.ds(r * rows_half, rows_half)
+        row = pl.ds(r * rows_part, rows_part)
         hb[row, :] = hb[row, :] + ((pb[layer, row, :] + recv_l[layer, row, :]) + recv_r[layer, row, :])
 
     rs = scatter_copies(0)
@@ -421,7 +436,7 @@
     norm_rows(hidden_row, ROW_FFN, mb.at[0], OP * seq, seq)
     feed_forward(0, OP, 1)
     forward_context(OP)
-    for r in range(2):
+    for r in range(ROW_PARTS):
         rs["op_r", r].start()
         rs["op_l", r].start()
     for slot in (OWN, OP):
@@ -433,8 +448,9 @@
     add_context(RT, 2)
     norm_rows(hidden_row, ROW_FFN, mb.at[0], RT * seq, 2 * seq)
     feed_forward(0, RT, 2)
-    rs["plain_r", 0].start()
-    rs["plain_l", 0].start()
+    for r in range(ROW_PARTS // 2):
+        rs["plain_r", r].start()
+        rs["plain_l", r].start()
     forward_wo(1)
     c_r[RT][1].wait_recv()
     c_l[LT][0].wait_recv()
@@ -443,10 +459,11 @@
     add_context(OWN, 1)
     norm_rows(hidden_row, ROW_FFN, mb.at[0], OWN * seq, seq)
     feed_forward(0, OWN, 1)
-    pass_on(0, rs, 0)
-    rs["plain_r", 1].start()
-    rs["plain_l", 1].start()
-    pass_on(0, rs, 1)
+    for r in range(ROW_PARTS):
+        pass_on(0, rs, r)
+        if r < ROW_PARTS // 2:
+            rs["plain_r", ROW_PARTS // 2 + r].start()
+            rs["plain_l", ROW_PARTS // 2 + r].start()
     spread_far_wo(1)
     for load_copy, copy in zip(qkv_loads[1], qkv_push[1]):
         load_copy.wait()
@@ -458,31 +475,20 @@
     out_loads[1].wait()
     out_push[1].start()
 
-    def gather_copies(ref, r):
-        to_right = [remote(part(ref, OWN, r, c), part(ref, LT, r, c), right) for c in range(2)]
-        to_left = [remote(part(ref, OWN, r, c), part(ref, RT, r, c), left) for c in range(2)]
-        fr = remote(part(ref, LT, r, 0), part(ref, OP, r, 0), right)
-        fl = remote(part(ref, RT, r, 1), part(ref, OP, r, 1), left)
-        return to_right, to_left, fr, fl
-
-    n_gather = [gather_copies(mb.at[2], r) for r in range(2)]
-    for r in range(2):
+    n_gather = [gather_copies(mb.at[2], r) for r in range(ROW_PARTS)]
+    for r in range(ROW_PARTS):
         collect(0, rs, r)
-        norm_rows(hidden_row, 1, mb.at[2], r * rows_half, rows_half)
+        norm_rows(hidden_row, 1, mb.at[2], r * rows_part, rows_part)
         to_right, to_left, _, _ = n_gather[r]
         to_right[0].start()
         to_left[1].start()
         to_right[1].start()
         to_left[0].start()
 
-    def forward_gather(gather):
-        to_right, to_left, fr, fl = gather
-        to_right[0].wait_recv()
-        fr.start()
-        to_left[1].wait_recv()
-        fl.start()
-
-    forward_gather(n_gather[0])
+        if r >= 2:
+            forward_gather(n_gather[r - 2])
+
+    forward_gather(n_gather[ROW_PARTS - 2])
     for copy in qkv_push[1]:
         copy.wait_recv()
     for copies in c_r, c_l:
@@ -492,23 +498,23 @@
                 done.add(id(copy))
     project(1, mb.at[2], OWN, 1)
     attend(1, OWN, 1)
-    forward_gather(n_gather[1])
+    forward_gather(n_gather[ROW_PARTS - 1])
     share_wo_near(1)
     share_wo_far(1)
-    for r in range(2):
+    for r in range(ROW_PARTS):
         n_gather[r][0][1].wait_recv()
         n_gather[r][1][0].wait_recv()
     project(1, mb.at[2], RT, 2)
     attend(1, RT, 2)
     ctx_r = remote(cb.at[0, rows(RT), :], c1b.at[LT], right)
     ctx_l = remote(cb.at[0, rows(LT), :], c1b.at[RT], left)
-    half_rows = lambda r: pl.ds(r * rows_half, rows_half)
-
-    ctx_o = [remote(cb.at[0, pl.ds(OP * seq + r * rows_half, rows_half), :], c1b.at[OP, half_rows(r), :], opposite)
-             for r in range(2)]
+    part_rows = lambda r: pl.ds(r * rows_part, rows_part)
+
+    ctx_o = [remote(cb.at[0, pl.ds(OP * seq + r * rows_part, rows_part), :], c1b.at[OP, part_rows(r), :], opposite)
+             for r in range(ROW_PARTS)]
     ctx_r.start()
     ctx_l.start()
-    for r in range(2):
+    for r in range(ROW_PARTS):
         n_gather[r][2].wait_recv()
         n_gather[r][3].wait_recv()
     project(1, mb.at[2], OP, 1)
@@ -518,7 +524,7 @@
     wo_push[1].wait_recv()
 
     def add_second(src, context, r=None):
-        row = rows(OWN) if r is None else half_rows(r)
+        row = rows(OWN) if r is None else part_rows(r)
         for j in range(0, d_model, chip_cols):
             col = pl.ds(j, chip_cols)
             hb[row, col] += dot(context, wob[1, src, :, col])
@@ -529,11 +535,11 @@
         copy.wait_recv()
         add_second(slot, c1b[slot])
     wo_share[1][OP].wait_recv()
-    m_gather = [gather_copies(mb.at[1], r) for r in range(2)]
-    for r in range(2):
+    m_gather = [gather_copies(mb.at[1], r) for r in range(ROW_PARTS)]
+    for r in range(ROW_PARTS):
         ctx_o[r].wait_recv()
-        add_second(OP, c1b[OP, half_rows(r), :], r)
-        norm_rows(hidden_row, ROW_FFN + 1, mb.at[1], r * rows_half, rows_half)
+        add_second(OP, c1b[OP, part_rows(r), :], r)
+        norm_rows(hidden_row, ROW_FFN + 1, mb.at[1], r * rows_part, rows_part)
         to_right, to_left, _, _ = m_gather[r]
         to_right[0].start()
         to_left[1].start()
@@ -543,29 +549,33 @@
         copy.wait_recv()
     out_push[1].wait_recv()
     rs = scatter_copies(1)
+    for r in range(ROW_PARTS // 2):
+        forward_gather(m_gather[r])
     feed_forward(1, OWN, 1)
-    for r in range(2):
+    for r in range(ROW_PARTS // 2, ROW_PARTS):
         forward_gather(m_gather[r])
-    for r in range(2):
+    for r in range(ROW_PARTS):
         m_gather[r][0][1].wait_recv()
         m_gather[r][1][0].wait_recv()
     feed_forward(1, RT, 2)
-    rs["plain_r", 0].start()
-    rs["plain_l", 0].start()
-    for r in range(2):
+    for r in range(ROW_PARTS // 2):
+        rs["plain_r", r].start()
+        rs["plain_l", r].start()
+    for r in range(ROW_PARTS):
         m_gather[r][2].wait_recv()
         m_gather[r][3].wait_recv()
     feed_forward(1, OP, 1)
-    for r in range(2):
+    for r in range(ROW_PARTS):
         rs["op_r", r].start()
         rs["op_l", r].start()
-    rs["plain_r", 1].start()
-    rs["plain_l", 1].start()
-    for r in range(2):
+    for r in range(ROW_PARTS // 2, ROW_PARTS):
+        rs["plain_r", r].start()
+        rs["plain_l", r].start()
+    for r in range(ROW_PARTS):
         pass_on(1, rs, r)
-    for r in range(2):
+    for r in range(ROW_PARTS):
         collect(1, rs, r)
-        norm_rows(hidden_row, ROW_FINAL, out, r * rows_half, rows_half, masked=True)
+        norm_rows(hidden_row, ROW_FINAL, out, r * rows_part, rows_part, masked=True)
     for copy in sent:
         if id(copy) not in done:
             copy.wait_send()
@@ -607,8 +617,8 @@
         pltpu.VMEM((layers, seq, d_model // 2), F32),
         pltpu.VMEM((layers, seq, d_model), F32),
         pltpu.VMEM((layers, seq, d_model), F32),
-        pltpu.SemaphoreType.DMA((160 + 4 * groups,)),
-        pltpu.SemaphoreType.DMA((160 + 4 * groups,)),
+        pltpu.SemaphoreType.DMA((240 + 4 * groups,)),
+        pltpu.SemaphoreType.DMA((240 + 4 * groups,)),
         pltpu.SemaphoreType.DMA((32,)),
     ]
     return pl.pallas_call(

time: 97.4 us -> 102 us (1.047); the launches traced: 96 us -> 102 us
  Pallas kernels: 94.7 us -> 100 us
    pallas_call x1, Pallas kernels: 94.7 us -> 100 us  [encode(): pl.pallas_call(functools.partial(kernel, n, groups), out_shape=pltpu.VMEM...]
where the time goes in v10:
time: 102 us
  Pallas kernels  100 us (98%)
    pallas_call x1, Pallas kernels, encode(): pl.pallas_call(functools.partial(kernel, n, groups), out_shape=pltpu.VMEM...  100 us

profile of v10, /device:TPU:81, one launch (start us, length us, event | category | flops | bytes accessed | tf_op | source)
XLA Modules:
  0.0 101.9 jit_solution(16126126811823951423)
XLA Ops:
  0.7 100.5 %shard_map.127 = bf16[128,1024]{1,0:T(8,128)(2,1)S(1)} custom-call(s32[1,1]{1,0:T(1,128)} %bitcast.8.lengths_in, bf16[2,128]{1,0:T(2,128)(2,1)} %attn_gain_in.1, bf16[2,128]{1,0:T(2,128)(2,1)} %ffn_gain_in.1, bf16[1,128]{1,0:T(2,128)(2,1)} %bitcast.13, bf16[4,32]{1,0:T(4,128)(2,1)} %bitcast.12, bf16[1,128,1024]{2,1,0:T(8,128)(2,1)} %tok.1, ...), custom_call_target="tpu_custom_call" | custom-call | tf_op jit(solution)/shard_map/pallas_call | solution.py:624
  101.1 0.7 copy.15

commit v11 on v8

--- a/solution.py
+++ b/solution.py
@@ -83,8 +83,8 @@
         return ref.at[row, col]
 
     barrier = pltpu.get_barrier_semaphore()
-    for k in range(1, n):
-        pl.semaphore_signal(barrier, inc=1, device_id={"fsdp": lax.rem(me + k, n)}, device_id_type=MESH)
+    for device in (right, left, opposite, partner):
+        pl.semaphore_signal(barrier, inc=1, device_id={"fsdp": device}, device_id_type=MESH)
     for k in range(1, groups):
         pl.semaphore_signal(barrier, inc=1, device_id={"dp": lax.rem(group + k, groups)}, device_id_type=MESH)
 
@@ -112,7 +112,7 @@
     smalls[ROW_BIAS:ROW_BIAS + 1, :] = jnp.concatenate([table[i:i + 1] for i in range(table.shape[0])], axis=1)
     smalls[ROW_LEN:SMALL_ROWS, :] = jnp.broadcast_to(lengths[...].astype(F32), (SMALL_ROWS - ROW_LEN, LANES))
 
-    pl.semaphore_wait(barrier, n - 1 + groups - 1)
+    pl.semaphore_wait(barrier, 4 + groups - 1)
 
     def block_sends(src, dst):
         to_right = [remote(src(c), dst(LT, c), right) for c in range(2)]
@@ -132,9 +132,14 @@
         col = lambda c: pl.ds(pl.multiple_of(piece_col + c * (piece_cols // 2), LANES), piece_cols // 2)
         src = lambda c: wob.at[layer, OWN, pl.ds(piece_row, piece_rows), col(c)]
         dst = lambda slot, c: wob.at[layer, slot, pl.ds(piece_row, piece_rows), col(c)]
-        to_right, to_left = block_sends(src, dst)
         fr, fl = block_forwards(dst)
         piece = lambda slot, count: wob.at[layer, pl.ds(slot, count), pl.ds(piece_row, piece_rows), pl.ds(piece_col, piece_cols)]
+        if layer == 0:
+            to_right, to_left = block_sends(src, dst)
+            to_left = to_left[::-1]
+        else:
+            to_right = [remote(piece(OWN, 1), piece(LT, 1), right)]
+            to_left = [remote(piece(OWN, 1), piece(RT, 1), left)]
         spread = [[remote(piece(slot, count), piece(slot, count), lax.rem(group + k, groups), "dp") for k in range(1, groups)]
                   for slot, count in ((RT, 2), (OP, 1))]
         push = {s: remote(wob.at[layer, s, pl.ds(0, share), :], wob.at[layer, s, pl.ds(share, share), :], partner)
@@ -144,18 +149,18 @@
     wo_r, wo_l, wo_fr, wo_fl, wo_spread, wo_share = zip(*[wo_copies(layer) for layer in range(layers)])
 
     def start_wo(layer):
-        wo_r[layer][0].start()
-        wo_l[layer][1].start()
-        wo_r[layer][1].start()
-        wo_l[layer][0].start()
+        for copy_right, copy_left in zip(wo_r[layer], wo_l[layer]):
+            copy_right.start()
+            copy_left.start()
 
     def forward_wo(layer):
         wo_r[layer][0].wait_recv()
         wo_fr[layer].start()
-        wo_l[layer][1].wait_recv()
+        wo_l[layer][0].wait_recv()
         wo_fl[layer].start()
-        wo_r[layer][1].wait_recv()
-        wo_l[layer][0].wait_recv()
+        for copies in wo_r[layer], wo_l[layer]:
+            for copy in copies[1:]:
+                copy.wait_recv()
         for copy in wo_spread[layer][0]:
             copy.start()
 
@@ -176,7 +181,10 @@
             copy.wait_recv()
         wo_share[layer][OP].start()
 
-    small_sends = [remote(smalls, sm_all.at[me], lax.rem(me + k, n)) for k in range(1, n)]
+    core, chip = lax.rem(me, 2), me // 2
+    small_sends = [remote(smalls, sm_all.at[core, chip], device) for device in (right, left, opposite)]
+    small_push = remote(sm_all.at[core], sm_all.at[core], partner)
+    small_of = lambda device: (lax.rem(device, 2), device // 2)
     tok_src = lambda c: part(tokb, OWN, None, c)
     tok_dst = lambda slot, c: part(tokb, slot, None, c)
     tok_r, tok_l = block_sends(tok_src, tok_dst)
@@ -208,13 +216,16 @@
     out_loads[0].wait()
     out_push[0].start()
 
-    sm_all[me] = smalls[...]
+    sm_all[core, chip] = smalls[...]
     for copy in small_sends:
         copy.wait_recv()
+    small_push.start()
+    small_push.wait_recv()
     for k in range(n):
-        gainb[:, k * LANES:(k + 1) * LANES] = sm_all[k]
+        gainb[:, k * LANES:(k + 1) * LANES] = sm_all[k % 2, k // 2]
     for slot, device in ((OWN, me), (RT, right), (LT, left), (OP, opposite)):
-        lenb[slot] = jnp.broadcast_to(sm_all[device, ROW_LEN:ROW_LEN + 1, :], (8, LANES))
+        at_core, at_chip = small_of(device)
+        lenb[slot] = jnp.broadcast_to(sm_all[at_core, at_chip, ROW_LEN:ROW_LEN + 1, :], (8, LANES))
 
     def norm_rows(load_row, gain_row, dst, start, count, masked=False):
         step = 32
@@ -281,7 +292,8 @@
         table_lane = lax.broadcasted_iota(jnp.int32, (8, LANES), 1)
         own_lanes = table_row == table_lane // NUM_BUCKETS
         for pair, device in ((0, me), (1, partner)):
-            tables = jnp.where(own_lanes, sm_all[device, ROW_BIAS:ROW_BIAS + 1, :], 0.0)
+            at_core, at_chip = small_of(device)
+            tables = jnp.where(own_lanes, sm_all[at_core, at_chip, ROW_BIAS:ROW_BIAS + 1, :], 0.0)
             lines = dot(tables.astype(BF16), one_hot)
             for layer in range(layers):
                 for h in range(2):
@@ -459,27 +471,34 @@
     out_push[1].start()
 
     def gather_copies(ref, r):
-        to_right = [remote(part(ref, OWN, r, c), part(ref, LT, r, c), right) for c in range(2)]
-        to_left = [remote(part(ref, OWN, r, c), part(ref, RT, r, c), left) for c in range(2)]
+        split = (None,) if r == 0 else (0, 1)
+        to_right = [remote(part(ref, OWN, r, c), part(ref, LT, r, c), right) for c in split]
+        to_left = [remote(part(ref, OWN, r, c), part(ref, RT, r, c), left) for c in reversed(split)]
         fr = remote(part(ref, LT, r, 0), part(ref, OP, r, 0), right)
         fl = remote(part(ref, RT, r, 1), part(ref, OP, r, 1), left)
         return to_right, to_left, fr, fl
 
+    def start_gather(gather):
+        for copy_right, copy_left in zip(gather[0], gather[1]):
+            copy_right.start()
+            copy_left.start()
+
+    def wait_near(gather):
+        for copies in gather[0], gather[1]:
+            for copy in copies[1:]:
+                copy.wait_recv()
+
     n_gather = [gather_copies(mb.at[2], r) for r in range(2)]
     for r in range(2):
         collect(0, rs, r)
         norm_rows(hidden_row, 1, mb.at[2], r * rows_half, rows_half)
-        to_right, to_left, _, _ = n_gather[r]
-        to_right[0].start()
-        to_left[1].start()
-        to_right[1].start()
-        to_left[0].start()
+        start_gather(n_gather[r])
 
     def forward_gather(gather):
         to_right, to_left, fr, fl = gather
         to_right[0].wait_recv()
         fr.start()
-        to_left[1].wait_recv()
+        to_left[0].wait_recv()
         fl.start()
 
     forward_gather(n_gather[0])
@@ -496,8 +515,7 @@
     share_wo_near(1)
     share_wo_far(1)
     for r in range(2):
-        n_gather[r][0][1].wait_recv()
-        n_gather[r][1][0].wait_recv()
+        wait_near(n_gather[r])
     project(1, mb.at[2], RT, 2)
     attend(1, RT, 2)
     ctx_r = remote(cb.at[0, rows(RT), :], c1b.at[LT], right)
@@ -534,11 +552,7 @@
         ctx_o[r].wait_recv()
         add_second(OP, c1b[OP, half_rows(r), :], r)
         norm_rows(hidden_row, ROW_FFN + 1, mb.at[1], r * rows_half, rows_half)
-        to_right, to_left, _, _ = m_gather[r]
-        to_right[0].start()
-        to_left[1].start()
-        to_right[1].start()
-        to_left[0].start()
+        start_gather(m_gather[r])
     for copy in in_push[1]:
         copy.wait_recv()
     out_push[1].wait_recv()
@@ -547,8 +561,7 @@
     for r in range(2):
         forward_gather(m_gather[r])
     for r in range(2):
-        m_gather[r][0][1].wait_recv()
-        m_gather[r][1][0].wait_recv()
+        wait_near(m_gather[r])
     feed_forward(1, RT, 2)
     rs["plain_r", 0].start()
     rs["plain_l", 0].start()
@@ -585,7 +598,7 @@
         pltpu.VMEM(final_gain.shape, BF16),
         pltpu.VMEM(bias_table.shape, BF16),
         pltpu.VMEM((SMALL_ROWS, LANES), F32),
-        pltpu.VMEM((n, SMALL_ROWS, LANES), F32),
+        pltpu.VMEM((2, ring, SMALL_ROWS, LANES), F32),
         pltpu.VMEM((8, d_model), F32),
         pltpu.VMEM((ring, 8, LANES), F32),
         pltpu.VMEM((layers, 2, seq, 2 * seq), F32),

time: 97.4 us -> 98.7 us (1.013)
  Pallas kernels: 94.7 us -> 95.7 us
    pallas_call x1, Pallas kernels: 94.7 us -> 95.7 us  [encode(): pl.pallas_call(functools.partial(kernel, n, groups), out_shape=pltpu.VMEM...]
where the time goes in v11:
time: 98.7 us; the launch traced here: 97.1 us
  Pallas kernels  95.7 us (97%)
    pallas_call x1, Pallas kernels, encode(): pl.pallas_call(functools.partial(kernel, n, groups), out_shape=pltpu.VMEM...  95.7 us

profile of v11, /device:TPU:81, one launch (start us, length us, event | category | flops | bytes accessed | tf_op | source)
XLA Modules:
  0.0 97.1 jit_solution(10521763429011579960)
XLA Ops:
  0.7 95.7 %shard_map.127 = bf16[128,1024]{1,0:T(8,128)(2,1)S(1)} custom-call(s32[1,1]{1,0:T(1,128)} %bitcast.8.lengths_in, bf16[2,128]{1,0:T(2,128)(2,1)} %attn_gain_in.1, bf16[2,128]{1,0:T(2,128)(2,1)} %ffn_gain_in.1, bf16[1,128]{1,0:T(2,128)(2,1)} %bitcast.13, bf16[4,32]{1,0:T(4,128)(2,1)} %bitcast.12, bf16[1,128,1024]{2,1,0:T(8,128)(2,1)} %tok.1, ...), custom_call_target="tpu_custom_call" | custom-call | tf_op jit(solution)/shard_map/pallas_call | solution.py:627
  96.4 0.7 copy.15

commit v12 on v8

--- a/solution.py
+++ b/solution.py
@@ -209,6 +209,9 @@
     out_push[0].start()
 
     sm_all[me] = smalls[...]
+    forward_wo(0)
+    tok_r[1].start()
+    tok_l[0].start()
     for copy in small_sends:
         copy.wait_recv()
     for k in range(n):
@@ -297,9 +300,6 @@
     project(0, nb, OWN, 1)
     attend(0, OWN, 1)
 
-    forward_wo(0)
-    tok_r[1].start()
-    tok_l[0].start()
     tok_fr, tok_fl = block_forwards(tok_dst)
     tok_r[0].wait_recv()
     tok_fr.start()

time: 97.4 us -> 98.7 us (1.013); the launches traced: 96 us -> 98.6 us
  Pallas kernels: 94.7 us -> 97.3 us
    pallas_call x1, Pallas kernels: 94.7 us -> 97.3 us  [encode(): pl.pallas_call(functools.partial(kernel, n, groups), out_shape=pltpu.VMEM...]
where the time goes in v12:
time: 98.7 us; the launch traced here: 98.6 us
  Pallas kernels  97.3 us (99%)
    pallas_call x1, Pallas kernels, encode(): pl.pallas_call(functools.partial(kernel, n, groups), out_shape=pltpu.VMEM...  97.3 us

profile of v12, /device:TPU:81, one launch (start us, length us, event | category | flops | bytes accessed | tf_op | source)
XLA Modules:
  0.0 98.6 jit_solution(14666301125967808570)
XLA Ops:
  0.7 97.3 %shard_map.127 = bf16[128,1024]{1,0:T(8,128)(2,1)S(1)} custom-call(s32[1,1]{1,0:T(1,128)} %bitcast.8.lengths_in, bf16[2,128]{1,0:T(2,128)(2,1)} %attn_gain_in.1, bf16[2,128]{1,0:T(2,128)(2,1)} %ffn_gain_in.1, bf16[1,128]{1,0:T(2,128)(2,1)} %bitcast.13, bf16[4,32]{1,0:T(4,128)(2,1)} %bitcast.12, bf16[1,128,1024]{2,1,0:T(8,128)(2,1)} %tok.1, ...), custom_call_target="tpu_custom_call" | custom-call | tf_op jit(solution)/shard_map/pallas_call | solution.py:614
  97.9 0.7 copy.15

commit v13 on v11

--- a/solution.py
+++ b/solution.py
@@ -83,8 +83,8 @@
         return ref.at[row, col]
 
     barrier = pltpu.get_barrier_semaphore()
-    for device in (right, left, opposite, partner):
-        pl.semaphore_signal(barrier, inc=1, device_id={"fsdp": device}, device_id_type=MESH)
+    for k in range(1, n):
+        pl.semaphore_signal(barrier, inc=1, device_id={"fsdp": lax.rem(me + k, n)}, device_id_type=MESH)
     for k in range(1, groups):
         pl.semaphore_signal(barrier, inc=1, device_id={"dp": lax.rem(group + k, groups)}, device_id_type=MESH)
 
@@ -112,7 +112,7 @@
     smalls[ROW_BIAS:ROW_BIAS + 1, :] = jnp.concatenate([table[i:i + 1] for i in range(table.shape[0])], axis=1)
     smalls[ROW_LEN:SMALL_ROWS, :] = jnp.broadcast_to(lengths[...].astype(F32), (SMALL_ROWS - ROW_LEN, LANES))
 
-    pl.semaphore_wait(barrier, 4 + groups - 1)
+    pl.semaphore_wait(barrier, n - 1 + groups - 1)
 
     def block_sends(src, dst):
         to_right = [remote(src(c), dst(LT, c), right) for c in range(2)]
@@ -181,10 +181,7 @@
             copy.wait_recv()
         wo_share[layer][OP].start()
 
-    core, chip = lax.rem(me, 2), me // 2
-    small_sends = [remote(smalls, sm_all.at[core, chip], device) for device in (right, left, opposite)]
-    small_push = remote(sm_all.at[core], sm_all.at[core], partner)
-    small_of = lambda device: (lax.rem(device, 2), device // 2)
+    small_sends = [remote(smalls, sm_all.at[me], lax.rem(me + k, n)) for k in range(1, n)]
     tok_src = lambda c: part(tokb, OWN, None, c)
     tok_dst = lambda slot, c: part(tokb, slot, None, c)
     tok_r, tok_l = block_sends(tok_src, tok_dst)
@@ -216,16 +213,13 @@
     out_loads[0].wait()
     out_push[0].start()
 
-    sm_all[core, chip] = smalls[...]
+    sm_all[me] = smalls[...]
     for copy in small_sends:
         copy.wait_recv()
-    small_push.start()
-    small_push.wait_recv()
     for k in range(n):
-        gainb[:, k * LANES:(k + 1) * LANES] = sm_all[k % 2, k // 2]
+        gainb[:, k * LANES:(k + 1) * LANES] = sm_all[k]
     for slot, device in ((OWN, me), (RT, right), (LT, left), (OP, opposite)):
-        at_core, at_chip = small_of(device)
-        lenb[slot] = jnp.broadcast_to(sm_all[at_core, at_chip, ROW_LEN:ROW_LEN + 1, :], (8, LANES))
+        lenb[slot] = jnp.broadcast_to(sm_all[device, ROW_LEN:ROW_LEN + 1, :], (8, LANES))
 
     def norm_rows(load_row, gain_row, dst, start, count, masked=False):
         step = 32
@@ -292,8 +286,7 @@
         table_lane = lax.broadcasted_iota(jnp.int32, (8, LANES), 1)
         own_lanes = table_row == table_lane // NUM_BUCKETS
         for pair, device in ((0, me), (1, partner)):
-            at_core, at_chip = small_of(device)
-            tables = jnp.where(own_lanes, sm_all[at_core, at_chip, ROW_BIAS:ROW_BIAS + 1, :], 0.0)
+            tables = jnp.where(own_lanes, sm_all[device, ROW_BIAS:ROW_BIAS + 1, :], 0.0)
             lines = dot(tables.astype(BF16), one_hot)
             for layer in range(layers):
                 for h in range(2):
@@ -598,7 +591,7 @@
         pltpu.VMEM(final_gain.shape, BF16),
         pltpu.VMEM(bias_table.shape, BF16),
         pltpu.VMEM((SMALL_ROWS, LANES), F32),
-        pltpu.VMEM((2, ring, SMALL_ROWS, LANES), F32),
+        pltpu.VMEM((n, SMALL_ROWS, LANES), F32),
         pltpu.VMEM((8, d_model), F32),
         pltpu.VMEM((ring, 8, LANES), F32),
         pltpu.VMEM((layers, 2, seq, 2 * seq), F32),

time: 98.7 us -> 97.4 us (0.987)
  Pallas kernels: 95.7 us -> 94.5 us
    pallas_call x1, Pallas kernels: 95.7 us -> 94.5 us  [encode(): pl.pallas_call(functools.partial(kernel, n, groups), out_shape=pltpu.VMEM...]
where the time goes in v13:
time: 97.4 us; the launch traced here: 95.9 us
  Pallas kernels  94.5 us (97%)
    pallas_call x1, Pallas kernels, encode(): pl.pallas_call(functools.partial(kernel, n, groups), out_shape=pltpu.VMEM...  94.5 us

profile of v13, /device:TPU:81, one launch (start us, length us, event | category | flops | bytes accessed | tf_op | source)
XLA Modules:
  0.0 95.9 jit_solution(4310319712311194890)
XLA Ops:
  0.7 94.5 %shard_map.127 = bf16[128,1024]{1,0:T(8,128)(2,1)S(1)} custom-call(s32[1,1]{1,0:T(1,128)} %bitcast.8.lengths_in, bf16[2,128]{1,0:T(2,128)(2,1)} %attn_gain_in.1, bf16[2,128]{1,0:T(2,128)(2,1)} %ffn_gain_in.1, bf16[1,128]{1,0:T(2,128)(2,1)} %bitcast.13, bf16[4,32]{1,0:T(4,128)(2,1)} %bitcast.12, bf16[1,128,1024]{2,1,0:T(8,128)(2,1)} %tok.1, ...), custom_call_target="tpu_custom_call" | custom-call | tf_op jit(solution)/shard_map/pallas_call | solution.py:620
  95.1 0.7 copy.15
